TPU v7x, 256 devices: a whole 4x4x8 slice. The times are simulated.
256 devices in a mesh: pop: 64 (over x, z, core), mp: 4 (over y).
Axes of the slice: x: 4, y: 4, z: 8, core: 2. Of those that a mesh axis runs over, the one named last changes fastest.
Arguments:
- tokens: bfloat16 [256, 3584], replicated, may hold values from -60 to 60
- target: bfloat16 [256, 3584], P(None, 'mp'), may hold values from -6 to 6
- w_query: bfloat16 [3584, 3584], P('pop', 'mp'), may hold values from -0.09375 to 0.09375
- w_key: bfloat16 [3584, 512], P(None, 'mp'), may hold values from -0.09375 to 0.09375
- w_value: bfloat16 [3584, 512], P(None, 'mp'), may hold values from -0.09375 to 0.09375
- w_out: bfloat16 [3584, 3584], P('mp', 'pop'), may hold values from -0.09375 to 0.09375
- query_left_factors: bfloat16 [64, 3584, 4], P('pop'), may hold values from -0.09375 to 0.09375
- query_right_factors: bfloat16 [64, 4, 3584], P('pop', None, 'mp'), may hold values from -6 to 6
- o_left: bfloat16 [64, 3584, 4], P('pop', 'mp'), may hold values from -0.09375 to 0.09375
- o_right: bfloat16 [64, 4, 3584], P('pop'), may hold values from -6 to 6
- member_ids: int32 [64], P('pop'), may hold values from 0 to 63, each once
Outputs:
- grad_query: float32 [3584, 3584], P('pop', 'mp')
- grad_out: float32 [3584, 3584], P('mp', 'pop')
- fitness: float32 [64], P('pop')
Inputs may be any that keep to these rules, and one draw needn't show every extreme that they name: `member_ids`: every number from 0 to 63 appears once.
All inputs are finite; a program needn't handle non-finite values.
Results may differ from a plain program's by a relative error of at most 0.005.
Values may be sent and summed in bfloat16 or wider, within the bound.
A program may use at most 64 MiB of HBM per device.

v0:
```python
import math

import jax
import jax.numpy as jnp
from jax import lax
from jax.sharding import Mesh
from jax.sharding import PartitionSpec as P

D = 3584
HEADS = 28
KV_HEADS = 4
HEAD_DIM = 128
RANK = 4
POP = ("pop_0", "pop_1", "pop_2")


noise_scale = 0.5
rope_base = 1000000.0
spread_floor = 0.001


def in_order(parts, dim):
    parts = jnp.moveaxis(parts, 0, dim)
    shape = parts.shape
    return parts.reshape(*shape[:dim], shape[dim] * shape[dim + 1], *shape[dim + 2 :])


def all_blocks(shard, axes, turns):
    parts = shard[None]
    for k in turns:
        parts = lax.all_gather(parts, axes[k], axis=0, tiled=True)
    held = [lax.axis_size(axes[k]) for k in reversed(turns)]
    parts = parts.reshape(*held, *shard.shape)
    turned = sorted(range(len(turns)), key=lambda place: turns[len(turns) - 1 - place])
    return parts.transpose(*turned, *range(len(turns), parts.ndim)).reshape(-1, *shard.shape)


def whole_of(shard, axes, turns, dim):
    return in_order(all_blocks(shard, axes, turns), dim)


def cut_along(shard, dim, devices):
    before, after = (shard.shape[:dim], shard.shape[dim + 1 :])
    return jnp.moveaxis(shard.reshape(*before, devices, -1, *after), dim, 0)


def summed_on_arrival(shard, axis, dim):
    devices = lax.axis_size(axis)
    parts = lax.all_to_all(cut_along(shard, dim, devices), axis, 0, 0, tiled=True)
    return jnp.sum(parts.astype(jnp.float32), axis=0)


def copy_for_each(shard, axis):
    copies = jnp.broadcast_to(shard, (lax.axis_size(axis), *shard.shape))
    return lax.all_to_all(copies, axis, split_axis=0, concat_axis=0, tiled=True)


def of_everyone(shard, axis):
    return copy_for_each(shard, axis).sum(axis=0)


def gathered_copies(shard, axis, dim):
    return in_order(copy_for_each(shard, axis), dim)


def side_by_side(arrays, axis, dim, along):
    columns = [a.reshape(*a.shape[:along], -1) for a in arrays]
    both = jnp.concatenate(columns, axis=along)
    result, at, done = (lax.all_gather(both, axis, axis=dim, tiled=True), 0, [])
    for a, column in zip(arrays, columns):
        share = result[..., at : at + column.shape[along]]
        done.append(share.reshape(*share.shape[:along], *a.shape[along:]))
        at += column.shape[along]
    return tuple(done)


def tables(count, head_size):
    position = jnp.arange(count, dtype=jnp.float32)
    index = jnp.arange(head_size // 2, dtype=jnp.float32)
    freq = jnp.exp(-math.log(rope_base) * 2.0 * index / head_size)
    angle = position[:, None] * freq[None, :]
    return (jnp.cos(angle)[:, None, :], jnp.sin(angle)[:, None, :])


def rotate(field, cosine_table, sine):
    half = field.shape[-1] // 2
    first = field[..., :half]
    second = field[..., half:]
    return jnp.concatenate(
        [first * cosine_table - second * sine, second * cosine_table + first * sine], axis=-1
    )


def per_device(
    tokens,
    target,
    w_query,
    w_key,
    w_value,
    w_out,
    query_left_factors,
    query_right_factors,
    o_left,
    o_right,
    member_ids,
):
    tok = tokens.shape[0]
    local_feats = w_query.shape[1]
    local_kv = w_key.shape[1] // HEAD_DIM
    group = HEADS // KV_HEADS
    local_heads = local_kv * group
    slots = query_left_factors.shape[0]
    scale = HEAD_DIM ** (-0.5)
    cosine_table, sine = tables(tok, HEAD_DIM)
    base = jnp.dot(tokens, whole_of(w_query, POP, (0, 1, 2), 0), preferred_element_type=jnp.float32)
    keys = rotate(
        jnp.dot(tokens, w_key, preferred_element_type=jnp.float32).reshape(tok, local_kv, HEAD_DIM),
        cosine_table,
        sine,
    ).astype(jnp.bfloat16)
    values = (
        jnp.dot(tokens, w_value, preferred_element_type=jnp.float32)
        .astype(jnp.bfloat16)
        .reshape(tok, local_kv, HEAD_DIM)
    )
    signs = (1 - 2 * (member_ids % 2)).astype(jnp.float32)
    factor = noise_scale * signs[:, None, None]
    lowrank_product = jnp.einsum(
        "td,mdr->mtr", tokens, query_left_factors, preferred_element_type=jnp.float32
    ).astype(jnp.bfloat16)
    query = base[None] + factor * jnp.einsum(
        "olj,ojv->olv", lowrank_product, query_right_factors, preferred_element_type=jnp.float32
    )
    query = rotate(
        query.reshape(slots, tok, local_heads, HEAD_DIM), cosine_table[None], sine[None]
    ).astype(jnp.bfloat16)
    query = query.reshape(slots, tok, local_kv, group, HEAD_DIM)
    scores = jnp.einsum("mtkgd,skd->mkgts", query, keys, preferred_element_type=jnp.float32) * scale
    causal = jnp.arange(tok)[:, None] >= jnp.arange(tok)[None, :]
    scores = jnp.where(causal, scores, -1e30)
    probs = jax.nn.softmax(scores, axis=-1).astype(jnp.bfloat16)
    mixed = (
        jnp.einsum("mkgts,skd->mtkgd", probs, values, preferred_element_type=jnp.float32)
        .astype(jnp.bfloat16)
        .reshape(slots, tok, local_feats)
    )
    low_out = jnp.einsum("mtf,mfr->mtr", mixed, o_left, preferred_element_type=jnp.float32)
    right_full = o_right.astype(jnp.float32)
    part = jnp.einsum(
        "mtf,fe->mte",
        mixed,
        lax.all_gather(w_out, POP, axis=1, tiled=True),
        preferred_element_type=jnp.float32,
    )
    term = part + factor * jnp.einsum(
        "mtr,mre->mte", low_out, right_full, precision=lax.Precision.HIGHEST
    )
    output = summed_on_arrival(term.astype(jnp.bfloat16), "mp", 2)
    diff = output - target.astype(jnp.float32)[None]
    errors = of_everyone(jnp.sum(diff * diff, axis=(1, 2)), "mp")
    fitness = -(errors / (tok * D))
    count = slots * lax.axis_size(POP)
    everyone = gathered_copies(fitness, POP, 0)
    mean = jnp.sum(everyone) / count
    spread = jnp.sum((everyone - mean) * (everyone - mean)) / count
    weight = signs * (fitness - mean) / jnp.sqrt(spread + spread_floor)
    every_weight = gathered_copies(weight, POP, 0)
    right_factors_gathered, left_all = side_by_side((query_right_factors, o_left), POP, 0, 1)
    rows_q = lax.all_to_all(query_left_factors, POP, split_axis=1, concat_axis=0, tiled=True)
    cols_o = lax.all_to_all(o_right, POP, split_axis=2, concat_axis=0, tiled=True)
    whole_population = rows_q.shape[0]
    left_q = jnp.transpose(
        rows_q.astype(jnp.float32) * every_weight[:, None, None], (1, 0, 2)
    ).reshape(rows_q.shape[1], whole_population * RANK)
    right_q = right_factors_gathered.astype(jnp.float32).reshape(
        whole_population * RANK, local_feats
    )
    grad_query = jnp.dot(left_q, right_q, precision=lax.Precision.HIGHEST) / noise_scale
    output_left_factor = jnp.transpose(
        left_all.astype(jnp.float32) * every_weight[:, None, None], (1, 0, 2)
    ).reshape(local_feats, whole_population * RANK)
    right_o = cols_o.astype(jnp.float32).reshape(whole_population * RANK, cols_o.shape[2])
    grad_out = jnp.dot(output_left_factor, right_o, precision=lax.Precision.HIGHEST) / noise_scale
    return (grad_query, grad_out, fitness)


def solution(mesh):
    torus = Mesh(mesh.devices.reshape(4, 8, 2, mesh.shape["mp"]), ("pop_0", "pop_1", "pop_2", "mp"))
    placed = (
        P(),
        P(None, "mp"),
        P(POP, "mp"),
        P(None, "mp"),
        P(None, "mp"),
        P("mp", POP),
        P(POP, None, None),
        P(POP, None, "mp"),
        P(POP, "mp", None),
        P(POP, None, None),
        P(POP),
    )
    return jax.shard_map(
        per_device,
        mesh=torus,
        in_specs=placed,
        out_specs=(P(POP, "mp"), P("mp", POP), P(POP)),
        check_vma=False,
    )
```

profile of v0, /device:TPU:1, one launch (start us, length us, event | category | flops | bytes accessed | tf_op | source)
XLA Modules:
  0.0 428.7 jit_solution(7784847421207332163)
XLA Ops:
  7.2 13.0 %all-gather = bf16[224,896]{1,0:T(8,128)(2,1)} all-gather(bf16[56,896]{1,0:T(8,128)(2,1)} %param.13), channel_id=2, replica_groups=mesh['pop_0'=4,'pop_1'=8,'pop_2'=2,'mp'=4] {'pop_0'}, dimensions={0}, use_global_device_ids=true | all-gather | bytes 501760 | tf_op jit(solution)/shard_map/all_gather | solution.py:31
  20.3 49.6 %all-gather.6.cloned.1.call-done = bf16[32,56,896]{2,1,0:T(8,128)(2,1)} async-done(((bf16[4,56,896]{2,1,0:T(8,128)(2,1)}), bf16[32,56,896]{2,1,0:T(8,128)(2,1)}) %all-gather.6.cloned.1.call-update) | async-done | bytes 3211280 | tf_op jit(solution)/shard_map/all_gather | solution.py:31
  70.0 0.7 all-gather.10.cloned.1.call-update
  71.4 0.7 convolution_bitcast_fusion
  72.2 1.0 fusion.18
  73.6 19.9 %all-gather.8.cloned.1.call-done = bf16[64,56,896]{2,1,0:T(8,128)(2,1)} async-done(((bf16[32,56,896]{2,1,0:T(8,128)(2,1)}), bf16[64,56,896]{2,1,0:T(8,128)(2,1)}) %all-gather.8.cloned.1.call-update) | async-done | bytes 6422544 | tf_op jit(solution)/shard_map/all_gather | solution.py:31
  93.5 3.3 copy.114
  96.9 2.1 fusion.29
  99.1 2.1 fusion.3
  101.1 1.5 copy.115
  102.6 0.9 fusion.27
  103.5 1.3 copy.140
  104.8 1.3 copy.141
  106.1 1.4 fusion.7
  108.2 1.2 copy-done.2
  110.0 2.6 convolution_convert_fusion
  112.8 65.1 %all-gather.10.cloned.1.call-done = bf16[896,3584]{0,1:T(8,128)(2,1)} async-done(((bf16[896,56]{0,1:T(8,128)(2,1)}), bf16[896,3584]{0,1:T(8,128)(2,1)}) %all-gather.10.cloned.1.call-update) | async-done | bytes 6422544 | tf_op jit(solution)/shard_map/all_gather | solution.py:152
  177.9 4.9 %fusion.30 = f32[256,3584]{1,0:T(8,128)S(1)} fusion(bf16[256,896]{0,1:T(8,128)(2,1)S(1)} %bitcast.106, bf16[896,3584]{0,1:T(8,128)(2,1)} %all-gather.10.cloned.1.call-done), kind=kOutput, calls=%fused_computation.58 | convolution fusion | flops 1644167168 | bytes 10551296 | tf_op jit(solution)/shard_map/mtf,fe->mte/dot_general | solution.py:149
  182.8 3.1 fusion.1
  185.9 3.3 reshape.288
  189.2 1.5 copy.145
  190.7 4.0 all-to-all-start.1
  195.3 22.5 %all-to-all-done.1 = bf16[4,1,256,896]{3,2,1,0:T(8,128)(2,1)S(1)} async-done(((bf16[4,1,256,896]{3,2,1,0:T(8,128)(2,1)}), bf16[4,1,256,896]{3,2,1,0:T(8,128)(2,1)S(1)}, u32[]{:S(2)}, u32[]{:S(2)}) %all-to-all-start.1) | async-done | bytes 1835040 | tf_op jit(solution)/shard_map/all_to_all | solution.py:49
  218.1 0.9 multiply_reduce_fusion
  218.9 0.6 broadcast_in_dim.34
  219.6 6.5 %all_to_all.47 = f32[4,1,1]{2,1,0:T(1,128)S(1)} all-to-all(f32[4,1,1]{2,1,0:T(1,128)S(1)} %broadcast_in_dim.34), channel_id=1, replica_groups=mesh['pop_0'=4,'pop_1'=8,'pop_2'=2,'mp'=4] {'mp'}, dimensions={0} | all-to-all | bytes 32 | tf_op jit(solution)/shard_map/all_to_all | solution.py:55
  227.3 0.6 broadcast_in_dim.35
  227.9 7.9 %all-to-all-start.3 = ((f32[64,1,1]{2,1,0:T(1,128)}), f32[64,1,1]{2,1,0:T(1,128)S(1)}, u32[]{:S(2)}, u32[]{:S(2)}) async-start(f32[64,1,1]{2,1,0:T(1,128)} %broadcast_in_dim.35), calls=%async_computation.3 | async-start | bytes 65536 | tf_op jit(solution)/shard_map/all_to_all | solution.py:55
  235.9 51.8 %all-gather.1 = bf16[64,1,7168]{2,1,0:T(2,128)(2,1)S(1)} all-gather(bf16[1,1,7168]{2,1,0:T(2,128)(2,1)S(1)} %maximum_bitcast_fusion.2), channel_id=1, replica_groups=mesh['pop_0'=4,'pop_1'=8,'pop_2'=2,'mp'=4] {'pop_0','pop_1','pop_2'}, dimensions={0}, use_global_device_ids=true | all-gather | bytes 931840 | tf_op jit(solution)/shard_map/all_gather | solution.py:69
  287.7 3.2 copy.129
  290.9 1.2 copy.146
  292.2 7.3 %all-to-all-start.5 = ((bf16[1,4,3584]{1,0,2:T(2,128)(2,1)}), bf16[1,4,3584]{1,0,2:T(2,128)(2,1)S(1)}, u32[]{:S(2)}, u32[]{:S(2)}) async-start(bf16[1,4,3584]{1,0,2:T(2,128)(2,1)} %copy.129), calls=%async_computation.5 | async-start | bytes 3670016 | tf_op jit(solution)/shard_map/all_to_all | solution.py:170
  299.4 2.0 slice_convert_fusion
  301.5 3.2 copy.112
  304.7 0.7 reduce_sum.58
  306.1 38.7 %all-to-all-done.5 = bf16[1,4,3584]{1,0,2:T(2,128)(2,1)S(1)} async-done(((bf16[1,4,3584]{1,0,2:T(2,128)(2,1)}), bf16[1,4,3584]{1,0,2:T(2,128)(2,1)S(1)}, u32[]{:S(2)}, u32[]{:S(2)}) %all-to-all-start.5) | async-done | bytes 28704 | tf_op jit(solution)/shard_map/all_to_all | solution.py:170
  344.8 6.2 %all-to-all-start = ((bf16[1,3584,4]{2,0,1:T(2,128)(2,1)}), bf16[1,3584,4]{2,0,1:T(2,128)(2,1)}, u32[]{:S(2)}, u32[]{:S(2)}) async-start(bf16[1,3584,4]{2,0,1:T(2,128)(2,1)} %copy.112), calls=%async_computation | async-start | bytes 3670016 | tf_op jit(solution)/shard_map/all_to_all | solution.py:169
  352.3 44.0 %all-to-all-done = bf16[1,3584,4]{2,0,1:T(2,128)(2,1)} async-done(((bf16[1,3584,4]{2,0,1:T(2,128)(2,1)}), bf16[1,3584,4]{2,0,1:T(2,128)(2,1)}, u32[]{:S(2)}, u32[]{:S(2)}) %all-to-all-start) | async-done | bytes 28704 | tf_op jit(solution)/shard_map/all_to_all | solution.py:169
  396.9 6.0 %all-to-all-start.4 = ((f32[64,1,1]{2,1,0:T(1,128)}), f32[64,1,1]{2,1,0:T(1,128)S(1)}, u32[]{:S(2)}, u32[]{:S(2)}) async-start(f32[64,1,1]{2,1,0:T(1,128)} %broadcast_in_dim.36), calls=%async_computation.4 | async-start | bytes 65536 | tf_op jit(solution)/shard_map/all_to_all | solution.py:55
  403.0 1.8 copy.127
  404.7 1.3 reshape.292
  406.0 1.8 copy.130
  408.1 3.7 copy.113
  412.8 1.6 multiply_bitcast_fusion
  414.4 2.8 copy.128
  417.2 1.5 reshape.293
  418.9 1.1 convolution_multiply_fusion.3
  420.0 1.1 convolution_multiply_fusion.2
  (55 shorter events, 6.1 us)
Async XLA Ops:
  7.2 64.2 %copy-start = (bf16[256,3584]{1,0:T(8,128)(2,1)S(1)}, bf16[256,3584]{1,0:T(8,128)(2,1)}, u32[]{:S(2)}) copy-start(bf16[256,3584]{1,0:T(8,128)(2,1)} %param.11) | copy-start | bytes 5505028
  7.2 62.7 %all-gather.6.cloned.1.call-start = ((), (), s32[]{:S(2)}) async-start(), calls=%async_computation.6 | async-start | bytes 3612672 | tf_op jit(solution)/shard_map/all_gather | solution.py:31
  20.2 51.2 %copy-start.4 = (bf16[3584,128]{1,0:T(8,128)(2,1)S(1)}, bf16[3584,128]{1,0:T(8,128)(2,1)}, u32[]{:S(2)}) copy-start(bf16[3584,128]{1,0:T(8,128)(2,1)} %param.14) | copy-start | bytes 2752516
  20.3 73.3 %all-gather.8.cloned.1.call-start = ((), (), s32[]{:S(2)}) async-start(), calls=%async_computation.7 | async-start | bytes 9633792 | tf_op jit(solution)/shard_map/all_gather | solution.py:31
  69.9 107.9 %all-gather.10.cloned.1.call-start = ((), (), s32[]{:S(2)}) async-start(), calls=%async_computation.8 | async-start | bytes 6522880 | tf_op jit(solution)/shard_map/all_gather | solution.py:152
  96.9 2.2 copy-start.9
  96.9 2.2 copy-start.11
  106.1 1.4 copy-start.6
  106.1 1.4 copy-start.7
  108.1 1.3 copy-start.2
  108.2 1.9 copy-start.13
  110.0 2.6 copy-start.12
  112.8 70.0 %copy-start.8 = (bf16[1,4,3584]{2,1,0:T(4,128)(2,1)S(1)}, bf16[1,4,3584]{2,1,0:T(4,128)(2,1)}, u32[]{:S(2)}) copy-start(bf16[1,4,3584]{2,1,0:T(4,128)(2,1)} %param.20) | copy-start | bytes 86020
  190.7 27.1 %all-to-all-start.1 = ((bf16[4,1,256,896]{3,2,1,0:T(8,128)(2,1)}), bf16[4,1,256,896]{3,2,1,0:T(8,128)(2,1)S(1)}, u32[]{:S(2)}, u32[]{:S(2)}) async-start(bf16[4,1,256,896]{3,2,1,0:T(8,128)(2,1)} %bitcast.98), calls=%async_computation.1 | async-start | bytes 3670016 | tf_op jit(solution)/shard_map/all_to_all | solution.py:49
  194.7 23.3 %copy-start.5 = (bf16[256,896]{1,0:T(8,128)(2,1)S(1)}, bf16[256,896]{1,0:T(8,128)(2,1)}, u32[]{:S(2)}) copy-start(bf16[256,896]{1,0:T(8,128)(2,1)} %param.12) | copy-start | bytes 1376260
  227.9 64.2 %all-to-all-start.3 = ((f32[64,1,1]{2,1,0:T(1,128)}), f32[64,1,1]{2,1,0:T(1,128)S(1)}, u32[]{:S(2)}, u32[]{:S(2)}) async-start(f32[64,1,1]{2,1,0:T(1,128)} %broadcast_in_dim.35), calls=%async_computation.3 | async-start | bytes 65536 | tf_op jit(solution)/shard_map/all_to_all | solution.py:55
  292.2 52.6 %all-to-all-start.5 = ((bf16[1,4,3584]{1,0,2:T(2,128)(2,1)}), bf16[1,4,3584]{1,0,2:T(2,128)(2,1)S(1)}, u32[]{:S(2)}, u32[]{:S(2)}) async-start(bf16[1,4,3584]{1,0,2:T(2,128)(2,1)} %copy.129), calls=%async_computation.5 | async-start | bytes 3670016 | tf_op jit(solution)/shard_map/all_to_all | solution.py:170
  299.4 2.1 copy-start.10
  344.8 51.5 %all-to-all-start = ((bf16[1,3584,4]{2,0,1:T(2,128)(2,1)}), bf16[1,3584,4]{2,0,1:T(2,128)(2,1)}, u32[]{:S(2)}, u32[]{:S(2)}) async-start(bf16[1,3584,4]{2,0,1:T(2,128)(2,1)} %copy.112), calls=%async_computation | async-start | bytes 3670016 | tf_op jit(solution)/shard_map/all_to_all | solution.py:169
  396.9 15.3 %all-to-all-start.4 = ((f32[64,1,1]{2,1,0:T(1,128)}), f32[64,1,1]{2,1,0:T(1,128)S(1)}, u32[]{:S(2)}, u32[]{:S(2)}) async-start(f32[64,1,1]{2,1,0:T(1,128)} %broadcast_in_dim.36), calls=%async_computation.4 | async-start | bytes 65536 | tf_op jit(solution)/shard_map/all_to_all | solution.py:55
  407.9 4.9 %copy-start.3 = (f32[64,3584]{0,1:T(8,128)S(1)}, f32[64,3584]{0,1:T(8,128)}, u32[]{:S(2)}) copy-start(f32[64,3584]{0,1:T(8,128)} %copy.127) | copy-start | bytes 2752516
  414.3 6.7 %copy-start.1 = (bf16[256,3584]{1,0:T(8,128)(2,1)S(1)}, bf16[256,3584]{1,0:T(8,128)(2,1)}, u32[]{:S(2)}) copy-start(bf16[256,3584]{1,0:T(8,128)(2,1)} %param.11) | copy-start | bytes 5505028
Sparse Core Ops, SparseCore 0:
  20.4 49.4 all-gather.5
  71.7 21.7 all-gather.7
  96.2 81.5 all-gather.9
where the time goes:
time: 430 us; the launch traced here: 429 us
  waiting for transfers between devices  241 us (56%)
  blocking collectives  71.3 us (17%)
  local copies, waits for them, and re-layouts  38.2 us (9%)
  starting transfers between devices  31.5 us (7%)
  matrix products  18.6 us (4%)
  between operations  17.9 us (4%)
  other arithmetic  10.5 us (2%)
    all_gather x2, waiting for transfers between devices, all_blocks(): parts = lax.all_gather(parts, axes[k], axis=0, tiled=True)  69.5 us
    all_gather x1, waiting for transfers between devices, per_device(): lax.all_gather(w_out, POP, axis=1, tiled=True)  65.1 us
    all_gather x1, blocking collectives, side_by_side(): result, at, done = (lax.all_gather(both, axis, axis=dim, tiled=True), 0, [])  51.8 us
    all_to_all x1, waiting for transfers between devices, per_device(): lax.all_to_all(query_left_factors, POP, split_axis=1, concat_axis=0, tile...  44 us
    all_to_all x1, waiting for transfers between devices, per_device(): lax.all_to_all(o_right, POP, split_axis=2, concat_axis=0, tiled=True)  38.7 us
    all_to_all x1, waiting for transfers between devices, summed_on_arrival(): lax.all_to_all(cut_along(shard, dim, devices), axis, 0, 0, tiled=True)  22.5 us
    all_to_all x2, starting transfers between devices, copy_for_each(): return lax.all_to_all(copies, axis, split_axis=0, concat_axis=0, tiled=True)  14 us
    all_gather x1, blocking collectives, all_blocks(): parts = lax.all_gather(parts, axes[k], axis=0, tiled=True)  13 us
  transfers between devices with their start and end apart: 8, of which 7 were waited for; matrix products, arithmetic and copies ran while one was open for 9% of the time, Pallas kernels for 0%

commit v1 on v0

v1 whole, which is shorter than its diff:
```python
import functools
import math

import jax
import jax.numpy as jnp
from jax import lax
from jax.experimental import pallas as pl
from jax.experimental.pallas import tpu as pltpu
from jax.sharding import Mesh
from jax.sharding import PartitionSpec as P

D = 3584
HEADS = 28
KV_HEADS = 4
HEAD_DIM = 128
RANK = 4
NX, NZ, NC, NY = 4, 8, 2, 4
PLANE = NX * NZ * NC
ROWS = D // PLANE
COLS = D // NY
AXES = ("pop_0", "pop_1", "pop_2", "mp")
POP = AXES[:3]
MESH = pl.DeviceIdType.MESH

noise_scale = 0.5
rope_base = 1000000.0
spread_floor = 0.001


def place():
    return tuple(lax.axis_index(a) for a in AXES)


def plane_device(p, y):
    return (p // (NZ * NC), (p // NC) % NZ, p % NC, y)


def meet_plane(me):
    x, z, c, y = me
    p = (x * NZ + z) * NC + c
    barrier = pltpu.get_barrier_semaphore()

    @pl.loop(1, PLANE)
    def _(i):
        pl.semaphore_signal(
            barrier, inc=1, device_id=plane_device((p + i) % PLANE, y), device_id_type=MESH
        )

    return barrier, PLANE - 1


def local_wait(ref, sem):
    pltpu.make_async_copy(ref, ref, sem).wait()


class PlaneGather:
    SEMS = 49

    def __init__(self, me, buf, sem, cut):
        self.x, self.z, self.c, self.y = me
        self.buf, self.sem = buf, sem
        self.a = pl.ds(0, cut)
        self.b = pl.ds(cut, COLS - cut)

    def zat(self, d):
        return (self.z + d + NZ) % NZ

    def xat(self, d):
        return (self.x + d + NX) % NX

    def send(self, ref, to, ssem, rsem):
        pltpu.make_async_remote_copy(
            src_ref=ref,
            dst_ref=ref,
            send_sem=self.sem.at[ssem],
            recv_sem=self.sem.at[rsem],
            device_id=to,
            device_id_type=MESH,
        ).start()

    def xdev(self, d):
        return (self.xat(d), self.z, self.c, self.y)

    def zdev(self, d):
        return (self.x, self.zat(d), self.c, self.y)

    def share(self, ref):
        self.send(ref, (self.x, self.z, 1 - self.c, self.y), 4, 5)

    def ra(self, right, s, h):
        return (7 if right else 15) + (s - 1) * 2 + h

    def rb(self, right, s):
        return (23 if right else 27) + s - 1

    def rx(self, right, k):
        return (31 if right else 39) + k

    @staticmethod
    def zoff(k):
        return -((k + 1) // 2) if k % 2 else k // 2

    def start(self):
        own_a = self.buf.at[self.x, self.z, self.c, :, self.a]
        own_b = self.buf.at[self.x, self.z, self.c, :, self.b]
        for d in (1, 3, 2):
            self.send(own_a, self.xdev(d), 0, 6)
        self.send(own_b, self.zdev(1), 2, self.rb(True, 1))
        self.send(own_b, self.zdev(-1), 2, self.rb(False, 1))
        self.send(own_b, self.xdev(1), 3, self.rx(True, 0))
        self.send(own_b, self.xdev(-1), 3, self.rx(False, 0))
        self.share(own_b)

    def a_line(self):
        local_wait(self.buf.at[pl.ds(0, 3), self.z, self.c, :, self.a], self.sem.at[6])
        for h in range(2):
            ref = self.buf.at[pl.ds(2 * h, 2), self.z, self.c, :, self.a]
            self.send(ref, self.zdev(1), 1, self.ra(True, 1, h))
            self.send(ref, self.zdev(-1), 1, self.ra(False, 1, h))
        self.share(self.buf.at[:, self.z, self.c, :, self.a])

    @staticmethod
    def a_moves(right, s, h):
        return s < 4 or (s == 4 and h == (0 if right else 1))

    def a_step(self, s):
        for h in range(2):
            for right in (True, False):
                if not self.a_moves(right, s, h):
                    continue
                zz = self.zat(-s if right else s)
                ref = self.buf.at[pl.ds(2 * h, 2), zz, self.c, :, self.a]
                local_wait(ref, self.sem.at[self.ra(right, s, h)])
                if s < 4 and self.a_moves(right, s + 1, h):
                    self.send(ref, self.zdev(1 if right else -1), 1, self.ra(right, s + 1, h))
                self.share(ref)

    def b_step(self, s):
        for right in (True, False):
            if s == 4 and not right:
                continue
            zz = self.zat(-s if right else s)
            k = 2 * s - 1 if right else 2 * s
            ref = self.buf.at[self.x, zz, self.c, :, self.b]
            local_wait(ref, self.sem.at[self.rb(right, s)])
            if s < 3 or (s == 3 and right):
                self.send(ref, self.zdev(1 if right else -1), 2, self.rb(right, s + 1))
            self.send(ref, self.xdev(1), 3, self.rx(True, k))
            self.send(ref, self.xdev(-1), 3, self.rx(False, k))
            self.share(ref)

    def x_step(self, k):
        zz = self.zat(self.zoff(k))
        for right in (True, False):
            ref = self.buf.at[self.xat(-1 if right else 1), zz, self.c, :, self.b]
            local_wait(ref, self.sem.at[self.rx(right, k)])
            if (k % 2 == 0) == right:
                self.send(ref, self.xdev(1 if right else -1), 3, 47 if right else 48)
            self.share(ref)

    def far(self):
        for s in (47, 48):
            local_wait(self.buf.at[0, pl.ds(0, 4), self.c, :, self.b], self.sem.at[s])
        self.share(self.buf.at[self.xat(2), :, self.c, :, self.b])

    def finish(self):
        local_wait(self.buf.at[:, :, 1 - self.c], self.sem.at[5])

    def drain(self):
        local_wait(self.buf.at[pl.ds(0, 3), 0, 0, :, self.a], self.sem.at[0])
        local_wait(self.buf.at[:, pl.ds(0, 7), 0, :, self.a], self.sem.at[1])
        local_wait(self.buf.at[0, pl.ds(0, 7), 0, :, self.b], self.sem.at[2])
        local_wait(self.buf.at[pl.ds(0, 3), :, 0, :, self.b], self.sem.at[3])
        local_wait(self.buf.at[:, :, self.c], self.sem.at[4])

    def run(self):
        self.a_line()
        for s in range(1, 5):
            self.b_step(s)
            for k in ((0,), (1, 2), (3, 4), (5, 6))[s - 1]:
                self.x_step(k)
            self.a_step(s)
        self.x_step(7)
        self.far()
        self.finish()


CUT = 384


def gather_kernel(wq, fac, wo, s_in, g1, g2, s_out, sem1, sem2, sem_s, sem_l):
    me = place()
    x, z, c, y = me
    p = (x * NZ + z) * NC + c
    barrier, expected = meet_plane(me)
    own = [
        pltpu.make_async_copy(wq, g1.at[x, z, c, pl.ds(0, ROWS), :], sem_l.at[0]),
        pltpu.make_async_copy(fac, g1.at[x, z, c, pl.ds(ROWS, 8), :], sem_l.at[1]),
        pltpu.make_async_copy(wo, g2.at[x, z, c], sem_l.at[2]),
    ]
    for copy in own:
        copy.start()
    s_out[p] = s_in[p]
    for copy in own:
        copy.wait()
    pl.semaphore_wait(barrier, expected)
    first = PlaneGather(me, g1, sem1, CUT)
    second = PlaneGather(me, g2, sem2, CUT)
    first.start()

    @pl.loop(1, PLANE)
    def _(i):
        to = (p + i) % PLANE
        pltpu.make_async_remote_copy(
            src_ref=s_in.at[to],
            dst_ref=s_out.at[p],
            send_sem=sem_s.at[0],
            recv_sem=sem_s.at[1],
            device_id=plane_device(to, y),
            device_id_type=MESH,
        ).start()

    second.start()
    first.run()
    second.run()
    local_wait(s_out.at[pl.ds(0, PLANE - 1)], sem_s.at[1])
    local_wait(s_out.at[pl.ds(0, PLANE - 1)], sem_s.at[0])
    first.drain()
    second.drain()


def gather_all(wq, fac, wo, s_in):
    return pl.pallas_call(
        gather_kernel,
        name="gather_all",
        out_shape=(
            jax.ShapeDtypeStruct((NX, NZ, NC, ROWS + 8, COLS), jnp.bfloat16),
            jax.ShapeDtypeStruct((NX, NZ, NC, ROWS, COLS), jnp.bfloat16),
            jax.ShapeDtypeStruct(s_in.shape, s_in.dtype),
        ),
        in_specs=[pl.BlockSpec(memory_space=pl.ANY)] * 3 + [pl.BlockSpec(memory_space=pltpu.VMEM)],
        out_specs=[pl.BlockSpec(memory_space=pltpu.VMEM)] * 3,
        scratch_shapes=[
            pltpu.SemaphoreType.DMA((PlaneGather.SEMS,)),
            pltpu.SemaphoreType.DMA((PlaneGather.SEMS,)),
            pltpu.SemaphoreType.DMA((2,)),
            pltpu.SemaphoreType.DMA((3,)),
        ],
        compiler_params=pltpu.CompilerParams(
            collective_id=0, has_side_effects=True, vmem_limit_bytes=56 * 1024 * 1024
        ),
    )(wq, fac, wo, s_in)


def exchange_kernel(t_ref, r_ref, fwd, ssem, rsem):
    x, z, c, y = place()
    up, down, far = (y + 1) % NY, (y + NY - 1) % NY, (y + 2) % NY
    half = COLS // 2
    lo, hi = pl.ds(0, half), pl.ds(half, half)
    barrier = pltpu.get_barrier_semaphore()
    for to in (up, down):
        pl.semaphore_signal(barrier, inc=1, device_id=(x, z, c, to), device_id_type=MESH)
    pl.semaphore_wait(barrier, 2)

    def send(src, dst, to, k):
        copy = pltpu.make_async_remote_copy(
            src_ref=src,
            dst_ref=dst,
            send_sem=ssem.at[k],
            recv_sem=rsem.at[k],
            device_id=(x, z, c, to),
            device_id_type=MESH,
        )
        copy.start()
        return copy

    copies = [
        send(t_ref.at[far, lo], fwd.at[0], up, 0),
        send(t_ref.at[far, hi], fwd.at[1], down, 1),
        send(t_ref.at[up], r_ref.at[y], up, 2),
        send(t_ref.at[down], r_ref.at[y], down, 3),
    ]
    r_ref[y] = t_ref[y]
    copies[0].wait_recv()
    copies.append(send(fwd.at[0], r_ref.at[down, lo], up, 4))
    copies[1].wait_recv()
    copies.append(send(fwd.at[1], r_ref.at[up, hi], down, 5))
    for copy in copies[2:]:
        copy.wait_recv()
    for copy in copies:
        copy.wait_send()


def exchange(terms):
    tok = terms.shape[2]
    return pl.pallas_call(
        exchange_kernel,
        name="exchange",
        out_shape=jax.ShapeDtypeStruct(terms.shape, terms.dtype),
        in_specs=[pl.BlockSpec(memory_space=pltpu.VMEM)],
        out_specs=pl.BlockSpec(memory_space=pltpu.VMEM),
        scratch_shapes=[
            pltpu.VMEM((2, COLS // 2, tok), terms.dtype),
            pltpu.SemaphoreType.DMA((6,)),
            pltpu.SemaphoreType.DMA((6,)),
        ],
        compiler_params=pltpu.CompilerParams(collective_id=1, has_side_effects=True),
    )(terms)


def scores_kernel(e_ref, out_ref, part, total, sem):
    me = place()
    x, z, c, y = me
    p = (x * NZ + z) * NC + c
    barrier, expected = meet_plane(me)
    for d in range(1, NY):
        pl.semaphore_signal(barrier, inc=1, device_id=(x, z, c, (y + d) % NY), device_id_type=MESH)
    part[y] = e_ref[...]
    pl.semaphore_wait(barrier, expected + NY - 1)
    for d in range(1, NY):
        pltpu.make_async_remote_copy(
            src_ref=e_ref,
            dst_ref=part.at[y],
            send_sem=sem.at[0],
            recv_sem=sem.at[1],
            device_id=(x, z, c, (y + d) % NY),
            device_id_type=MESH,
        ).start()
    local_wait(part.at[pl.ds(0, NY - 1)], sem.at[1])
    total[...] = part[0] + part[1] + part[2] + part[3]
    out_ref[p] = total[...]

    @pl.loop(1, PLANE)
    def _(i):
        pltpu.make_async_remote_copy(
            src_ref=total,
            dst_ref=out_ref.at[p],
            send_sem=sem.at[2],
            recv_sem=sem.at[3],
            device_id=plane_device((p + i) % PLANE, y),
            device_id_type=MESH,
        ).start()

    local_wait(out_ref.at[pl.ds(0, PLANE - 1)], sem.at[3])
    local_wait(part.at[pl.ds(0, NY - 1)], sem.at[0])
    local_wait(out_ref.at[pl.ds(0, PLANE - 1)], sem.at[2])


def everyone_scores(errors):
    return pl.pallas_call(
        scores_kernel,
        name="everyone_scores",
        out_shape=jax.ShapeDtypeStruct((PLANE, 1, 128), jnp.float32),
        in_specs=[pl.BlockSpec(memory_space=pltpu.VMEM)],
        out_specs=pl.BlockSpec(memory_space=pltpu.VMEM),
        scratch_shapes=[
            pltpu.VMEM((NY, 1, 128), jnp.float32),
            pltpu.VMEM((1, 128), jnp.float32),
            pltpu.SemaphoreType.DMA((4,)),
        ],
        compiler_params=pltpu.CompilerParams(collective_id=2, has_side_effects=True),
    )(errors)


def tables(count, head_size):
    position = jnp.arange(count, dtype=jnp.float32)
    index = jnp.arange(head_size // 2, dtype=jnp.float32)
    freq = jnp.exp(-math.log(rope_base) * 2.0 * index / head_size)
    angle = position[:, None] * freq[None, :]
    return (jnp.cos(angle)[:, None, :], jnp.sin(angle)[:, None, :])


def rotate(field, cosine_table, sine):
    half = field.shape[-1] // 2
    first = field[..., :half]
    second = field[..., half:]
    return jnp.concatenate(
        [first * cosine_table - second * sine, second * cosine_table + first * sine], axis=-1
    )


def per_device(
    tokens,
    target,
    w_query,
    w_key,
    w_value,
    w_out,
    query_left_factors,
    query_right_factors,
    o_left,
    o_right,
    member_ids,
):
    tok = tokens.shape[0]
    group = HEADS // KV_HEADS
    scale = HEAD_DIM ** (-0.5)
    f32 = jnp.float32
    cosine_table, sine = tables(tok, HEAD_DIM)

    signs = (1 - 2 * (member_ids % 2)).astype(f32)
    q_left_t = jnp.transpose(query_left_factors[0])
    o_left_t = jnp.transpose(o_left[0])
    fac = jnp.concatenate([query_right_factors[0], o_left_t], axis=0)
    both = jnp.concatenate([q_left_t, o_right[0]], axis=0)
    s_in = jnp.transpose(both.reshape(2 * RANK, PLANE, ROWS), (1, 0, 2))
    s_in = jnp.pad(s_in, ((0, 0), (0, 0), (0, 128 - ROWS))) * signs.astype(jnp.bfloat16)
    g1, g2, s_out = gather_all(w_query, fac, jnp.transpose(w_out), s_in)
    g1 = g1.reshape(PLANE, ROWS + 8, COLS)
    wide = jnp.pad(tokens.reshape(tok, PLANE, ROWS), ((0, 0), (0, 0), (0, 8)))
    base = jnp.dot(
        wide.reshape(tok, -1), g1.reshape(-1, COLS), preferred_element_type=f32
    )
    keys = rotate(
        jnp.dot(tokens, w_key, preferred_element_type=f32).reshape(tok, 1, HEAD_DIM),
        cosine_table,
        sine,
    ).astype(jnp.bfloat16)[:, 0]
    values = jnp.dot(tokens, w_value, preferred_element_type=f32).astype(jnp.bfloat16)
    factor = noise_scale * signs[0]
    low_q = jnp.dot(tokens, query_left_factors[0], preferred_element_type=f32).astype(jnp.bfloat16)
    query = base + factor * jnp.dot(low_q, query_right_factors[0], preferred_element_type=f32)
    query = rotate(query.reshape(tok, group, HEAD_DIM), cosine_table, sine).astype(jnp.bfloat16)
    scores = jnp.einsum("tgd,sd->gts", query, keys, preferred_element_type=f32) * scale
    causal = jnp.arange(tok)[:, None] >= jnp.arange(tok)[None, :]
    scores = jnp.where(causal, scores, -1e30)
    probs = jax.nn.softmax(scores, axis=-1).astype(jnp.bfloat16)
    mixed = (
        jnp.einsum("gts,sd->gdt", probs, values, preferred_element_type=f32)
        .astype(jnp.bfloat16)
        .reshape(COLS, tok)
    )
    low_o = jnp.dot(o_left_t, mixed, preferred_element_type=f32)
    part = jnp.dot(g2.reshape(D, COLS), mixed, preferred_element_type=f32)
    term = part + factor * jnp.einsum(
        "re,rt->et", o_right[0].astype(f32), low_o, precision=lax.Precision.HIGHEST
    )
    arrived = exchange(term.astype(jnp.bfloat16).reshape(NY, COLS, tok))
    output = jnp.sum(arrived.astype(f32), axis=0)
    diff = output - jnp.transpose(target).astype(f32)
    errors = jnp.full((1, 128), jnp.sum(diff * diff), f32)
    everyone = -(everyone_scores(errors)[:, 0, 0] / (tok * D))
    p = (lax.axis_index(POP[0]) * NZ + lax.axis_index(POP[1])) * NC + lax.axis_index(POP[2])
    fitness = lax.dynamic_slice(everyone, (p,), (1,))
    mean = jnp.sum(everyone) / PLANE
    spread = jnp.sum((everyone - mean) * (everyone - mean)) / PLANE
    unsigned = (everyone - mean) / jnp.sqrt(spread + spread_floor)
    lefts = s_out[:, :, :ROWS].astype(f32) * unsigned[:, None, None]
    rights = g1[:, ROWS:].astype(f32)

    def gradient(left, right):
        return (
            lax.dot_general(
                left.reshape(-1, ROWS),
                right.reshape(-1, COLS),
                (((0,), (0,)), ((), ())),
                precision=lax.Precision.HIGHEST,
            )
            / noise_scale
        )

    grad_query = gradient(lefts[:, :RANK], rights[:, :RANK])
    grad_out = gradient(lefts[:, RANK:], rights[:, RANK:])
    return (grad_query, jnp.transpose(grad_out), fitness)


def solution(mesh):
    torus = Mesh(mesh.devices.reshape(NX, NZ, NC, NY), AXES)
    placed = (
        P(),
        P(None, "mp"),
        P(POP, "mp"),
        P(None, "mp"),
        P(None, "mp"),
        P("mp", POP),
        P(POP, None, None),
        P(POP, None, "mp"),
        P(POP, "mp", None),
        P(POP, None, None),
        P(POP),
    )
    return jax.shard_map(
        per_device,
        mesh=torus,
        in_specs=placed,
        out_specs=(P(POP, "mp"), P("mp", POP), P(POP)),
        check_vma=False,
    )
```

time: 430 us -> 177 us (0.41)
  waiting for transfers between devices: 241 us -> 0 us
  Pallas kernels: 0 us -> 118 us
  blocking collectives: 71.3 us -> 0 us
  starting transfers between devices: 31.5 us -> 0 us
  local copies, waits for them, and re-layouts: 38.2 us -> 17 us
  between operations: 17.9 us -> 2.96 us
  matrix products: 18.6 us -> 26.4 us
    all_gather x3 -> x0, waiting for transfers between devices: 135 us -> none  [the longest x2 69.5 us: all_blocks(): parts = lax.all_gather(parts, axes[k], axis=0, tiled=True)]
    pallas_call x0 -> x3, Pallas kernels: none -> 118 us  [the longest x1 73.8 us: gather_all(): pl.pallas_call(gather_kernel, name='gather_all', out_shape=(jax.ShapeDtyp...]
    all_to_all x5 -> x0, waiting for transfers between devices: 105 us -> none  [the longest x1 44 us: per_device(): lax.all_to_all(query_left_factors, POP, split_axis=1, concat_axis=0, tile...]
    all_gather x2 -> x0, blocking collectives: 64.8 us -> none  [the longest x1 51.8 us: side_by_side(): result, at, done = (lax.all_gather(both, axis, axis=dim, tiled=True), 0, [])]
    all_to_all x5 -> x0, starting transfers between devices: 31.4 us -> none  [the longest x2 14 us: copy_for_each(): return lax.all_to_all(copies, axis, split_axis=0, concat_axis=0, tiled=True)]
    reshape x5 -> x0, local copies, waits for them, and re-layouts: 7.88 us -> none  [the longest x2 4.8 us: cut_along(): return jnp.moveaxis(shard.reshape(*before, devices, -1, *after), dim, 0)]
    all_to_all x1 -> x0, blocking collectives: 6.47 us -> none  [copy_for_each(): return lax.all_to_all(copies, axis, split_axis=0, concat_axis=0, tiled=True)]
    transpose x3 -> x0, local copies, waits for them, and re-layouts: 6.26 us -> none  [the longest x1 3.34 us: all_blocks(): parts.transpose(*turned, *range(len(turns), parts.ndim))]
  transfers between devices with their start and end apart: 8 -> 0, of which waited for: 7 -> 0; matrix products, arithmetic and copies ran while one was open for 9% -> 0% of each run, Pallas kernels for 0% -> 0%
where the time goes in v1:
time: 177 us
  Pallas kernels  118 us (67%)
  matrix products  26.4 us (15%)
  local copies, waits for them, and re-layouts  17 us (10%)
  other arithmetic  11.8 us (7%)
  between operations  2.96 us (2%)
    pallas_call x1, Pallas kernels, gather_all(): pl.pallas_call(gather_kernel, name='gather_all', out_shape=(jax.ShapeDtyp...  73.8 us
    pallas_call x1, Pallas kernels, exchange(): pl.pallas_call(exchange_kernel, name='exchange', out_shape=jax.ShapeDtype...  26.3 us
    pallas_call x1, Pallas kernels, everyone_scores(): pl.pallas_call(scores_kernel, name='everyone_scores', out_shape=jax.Shape...  18.3 us
    unnamed x22, local copies, waits for them, and re-layouts  6.83 us
    dot_general x1, matrix products, per_device(): jnp.dot(wide.reshape(tok, -1), g1.reshape(-1, COLS), preferred_element_ty...  6.52 us
    dot_general x1, matrix products, per_device(): part = jnp.dot(g2.reshape(D, COLS), mixed, preferred_element_type=f32)  4.95 us

profile of v1, /device:TPU:1, one launch (start us, length us, event | category | flops | bytes accessed | tf_op | source)
XLA Modules:
  0.0 176.5 jit_solution(16712646186004839234)
XLA Ops:
  0.6 0.0 copy-start
  1.4 0.9 concatenate.27
  2.3 0.1 copy.36
  2.4 0.9 concatenate.28
  3.2 0.1 copy.37
  3.3 0.1 maximum_bitcast_fusion
  3.4 0.7 pad_multiply_fusion.s_in
  4.1 1.3 pad_maximum_fusion.fac
  5.4 73.8 %gather_all.1 = (bf16[4,8,2,64,896]{4,3,2,1,0:T(8,128)(2,1)}, bf16[4,8,2,56,896]{4,3,2,1,0:T(8,128)(2,1)}, bf16[64,8,128]{2,1,0:T(8,128)(2,1)}) custom-call(bf16[56,896]{1,0:T(8,128)(2,1)} %wq.1, bf16[8,896]{1,0:T(8,128)(2,1)} %pad_maximum_fusion.fac, bf16[56,896]{1,0:T(8,128)(2,1)} %bitcast.99, bf16[64,8,128]{2,1,0:T(8,128)(2,1)} %pad_multiply_fusion.s_in), custom_call_target="tpu_custom_call" | custom-call | tf_op jit(solution)/shard_map/gather_all/pallas_call | solution.py:233
  79.3 3.1 %copy.38 = bf16[256,3584]{0,1:T(8,128)(2,1)S(1)} copy(bf16[256,3584]{1,0:T(8,128)(2,1)} %param.11) | data formatting | bytes 3670016 | tf_op args[0]
  82.3 0.3 pad.9
  82.6 0.0 copy-start.1
  82.6 0.0 copy-start.5
  82.6 0.0 copy-start.7
  82.6 6.5 %fusion.54 = f32[256,896]{1,0:T(8,128)} fusion(bf16[256,4096]{0,1:T(8,128)(2,1)S(1)} %bitcast.92, bf16[4096,896]{1,0:T(8,128)(2,1)} %bitcast.90), kind=kOutput, calls=%fused_computation.73 | convolution fusion | flops 1879048192 | bytes 10354688 | tf_op jit(solution)/shard_map/dot_general | solution.py:411
  89.2 0.0 copy-done.1
  89.2 0.0 copy-done.7
  89.2 3.2 %fusion.5 = f32[256,896]{1,0:T(8,128)} fusion(f32[256,896]{1,0:T(8,128)} %fusion.54, bf16[256,3584]{1,0:T(8,128)(2,1)S(1)} %copy-done.1, f32[]{:T(128)} %bitcast.17, bf16[1,3584,4]{1,2,0:T(4,128)(2,1)S(1)} %copy-done.5, bf16[1,4,896]{2,1,0:T(4,128)(2,1)S(1)} %copy-done.7), kind=kOutput, calls=%fused_computation.11 | convolution fusion | flops 9634816 | bytes 3705860 | tf_op jit(solution)/shard_map/dot_general | solution.py:422
  92.4 2.4 %copy.39 = f32[256,896]{0,1:T(8,128)} copy(f32[256,896]{1,0:T(8,128)} %fusion.5) | data formatting | bytes 1835008 | tf_op jit(solution)/shard_map/add | solution.py:422
  94.9 2.0 %fusion.49 = (f32[256,7,64]{0,2,1:T(8,128)S(1)}, f32[256,7,64]{0,2,1:T(8,128)}) fusion(f32[256,7,128]{0,2,1:T(8,128)} %bitcast.95), kind=kLoop, calls=%fused_computation.70 | loop fusion | bytes 1835008 | tf_op jit(solution)/shard_map/slice | solution.py:376
  96.9 2.3 %copy.57 = f32[256,7,64]{2,0,1:T(8,128)} copy(f32[256,7,64]{0,2,1:T(8,128)} %get-tuple-element.16) | data formatting | bytes 917504
  99.1 1.2 copy.58
  100.4 0.5 fusion.27
  100.9 2.5 %subtract_convert_fusion = (bf16[256,7,64]{2,0,1:T(8,128)(2,1)S(1)}, bf16[256,7,64]{2,0,1:T(8,128)(2,1)}) fusion(f32[256,7,64]{2,0,1:T(8,128)} %copy.58, f32[256,7,64]{2,0,1:T(8,128)} %copy.57, f32[256,64]{1,0:T(8,128)S(1)} %get-tuple-element.22, f32[256,64]{1,0:T(8,128)S(1)} %get-tuple-element.21), kind=kLoop, calls=%fused_computation.27 | loop fusion | flops 917504 | bytes 1507328 | tf_op jit(solution)/shard_map/convert.1
  103.4 0.8 convolution_bitcast_fusion.2
  104.2 0.3 fusion.32
  104.5 3.1 %fusion.51 = (f32[7,256]{1,0:T(8,128)S(1)}, f32[7,256,256]{1,2,0:T(8,128)}) fusion(pred[256,256]{0,1:T(8,128)(4,1)S(1)} %iota_compare_fusion, bf16[256,7,64]{2,0,1:T(8,128)(2,1)} %get-tuple-element.14, bf16[256,7,64]{2,0,1:T(8,128)(2,1)S(1)} %get-tuple-element.13, bf16[256,64]{0,1:T(8,128)(2,1)S(1)} %get-tuple-element.20, ...), kind=kOutput, calls=%fused_computation.72 | convolution fusion | flops 120324352 | bytes 2432000 | tf_op jit(solution)/shard_map/sub | solution.py:427
  107.6 2.5 %convolution_convert_fusion = bf16[128,7,256]{2,0,1:T(8,128)(2,1)S(1)} fusion(f32[7,256,256]{1,2,0:T(8,128)} %get-tuple-element.24, f32[7,256]{1,0:T(8,128)S(1)} %get-tuple-element.23, bf16[256,3584]{1,0:T(8,128)(2,1)S(1)} %copy-done.1, bf16[3584,128]{1,0:T(8,128)(2,1)S(1)} %copy-done), kind=kOutput, calls=%fused_computation.12 | convolution fusion | flops 353501184 | bytes 5053440 | tf_op jit(solution)/shard_map/gts,sd->gdt/dot_general | solution.py:429
  110.1 0.0 copy-start.8
  110.1 0.0 copy-start.6
  110.1 5.0 %fusion.55 = f32[3584,256]{1,0:T(8,128)S(1)} fusion(bf16[3584,896]{1,0:T(8,128)(2,1)} %bitcast.102, bf16[896,256]{1,0:T(8,128)(2,1)S(1)} %bitcast.96), kind=kOutput, calls=%fused_computation.74 | convolution fusion | flops 1644167168 | bytes 10551296 | tf_op jit(solution)/shard_map/dot_general | solution.py:434
  115.1 0.2 fusion.37
  115.3 3.0 %fusion.3 = bf16[3584,256]{1,0:T(8,128)(2,1)} fusion(f32[3584,256]{1,0:T(8,128)S(1)} %fusion.55, f32[256,4]{0,1:T(4,128)S(1)} %fusion.37, f32[]{:T(128)} %bitcast.17, bf16[1,4,3584]{2,1,0:T(4,128)(2,1)S(1)} %copy-done.6), kind=kOutput, calls=%fused_computation.4 | convolution fusion | flops 46792704 | bytes 5537796 | tf_op jit(solution)/shard_map/re,rt->et/dot_general | solution.py:435
  118.3 26.3 %exchange.1 = bf16[4,896,256]{2,1,0:T(8,128)(2,1)} custom-call(bf16[4,896,256]{2,1,0:T(8,128)(2,1)} %bitcast.93), custom_call_target="tpu_custom_call" | custom-call | tf_op jit(solution)/shard_map/exchange/pallas_call | solution.py:296
  144.6 0.0 copy-start.3
  144.6 1.9 %convert_reduce_fusion = f32[896,256]{1,0:T(8,128)S(1)} fusion(bf16[4,896,256]{2,1,0:T(8,128)(2,1)} %exchange.1), kind=kLoop, calls=%fused_computation.5 | loop fusion | flops 1605632 | bytes 2752512 | tf_op jit(solution)/shard_map/reduce_sum | solution.py:439
  146.6 0.2 copy.46
  146.8 0.8 fusion.10
  147.6 1.2 broadcast_in_dim.12.e_ref
  148.8 18.3 %everyone_scores.1 = f32[64,1,128]{2,1,0:T(1,128)} custom-call(f32[1,128]{1,0:T(1,128)} %broadcast_in_dim.12.e_ref), custom_call_target="tpu_custom_call" | custom-call | tf_op jit(solution)/shard_map/everyone_scores/pallas_call | solution.py:350
  167.1 1.4 fusion.39
  169.1 1.4 multiply_reduce_fusion
  171.3 0.6 divide_reduce_fusion
  171.8 0.1 convert_multiply_fusion
  172.0 1.9 %fusion.48 = (bf16[64,4,896]{2,1,0:T(4,128)(2,1)S(1)}, bf16[64,4,896]{2,1,0:T(4,128)(2,1)S(1)}) fusion(bf16[64,64,896]{2,1,0:T(8,128)(2,1)} %bitcast.91), kind=kLoop, calls=%fused_computation.69 | loop fusion | bytes 1835008 | tf_op jit(solution)/shard_map/slice | solution.py:463
  173.9 1.1 fusion.6
  175.0 1.1 fusion.7
  176.0 0.5 constant_dynamic-slice_fusion
  (12 shorter events, 0.1 us)
Async XLA Ops:
  0.6 107.0 %copy-start = (bf16[3584,128]{1,0:T(8,128)(2,1)S(1)}, bf16[3584,128]{1,0:T(8,128)(2,1)}, u32[]{:S(2)}) copy-start(bf16[3584,128]{1,0:T(8,128)(2,1)} %param.15) | copy-start | bytes 2752516
  82.6 6.6 %copy-start.1 = (bf16[256,3584]{1,0:T(8,128)(2,1)S(1)}, bf16[256,3584]{1,0:T(8,128)(2,1)}, u32[]{:S(2)}) copy-start(bf16[256,3584]{1,0:T(8,128)(2,1)} %param.11) | copy-start | bytes 5505028
  82.6 6.6 %copy-start.5 = (bf16[1,3584,4]{1,2,0:T(4,128)(2,1)S(1)}, bf16[1,3584,4]{1,2,0:T(4,128)(2,1)}, u32[]{:S(2)}) copy-start(bf16[1,3584,4]{1,2,0:T(4,128)(2,1)} %param.17) | copy-start | bytes 86020
  82.6 6.5 %copy-start.7 = (bf16[1,4,896]{2,1,0:T(4,128)(2,1)S(1)}, bf16[1,4,896]{2,1,0:T(4,128)(2,1)}, u32[]{:S(2)}) copy-start(bf16[1,4,896]{2,1,0:T(4,128)(2,1)} %param.18) | copy-start | bytes 21508
  100.4 3.0 %copy-start.2 = (bf16[3584,128]{1,0:T(8,128)(2,1)S(1)}, bf16[3584,128]{1,0:T(8,128)(2,1)}, u32[]{:S(2)}) copy-start(bf16[3584,128]{1,0:T(8,128)(2,1)} %param.14) | copy-start | bytes 2752516
  110.1 5.0 %copy-start.8 = (bf16[1,896,4]{1,2,0:T(4,128)(2,1)S(1)}, bf16[1,896,4]{1,2,0:T(4,128)(2,1)}, u32[]{:S(2)}) copy-start(bf16[1,896,4]{1,2,0:T(4,128)(2,1)} %param.19) | copy-start | bytes 21508
  110.1 5.1 %copy-start.6 = (bf16[1,4,3584]{2,1,0:T(4,128)(2,1)S(1)}, bf16[1,4,3584]{2,1,0:T(4,128)(2,1)}, u32[]{:S(2)}) copy-start(bf16[1,4,3584]{2,1,0:T(4,128)(2,1)} %param.20) | copy-start | bytes 86020
  144.6 1.9 %copy-start.3 = (bf16[256,896]{1,0:T(8,128)(2,1)S(1)}, bf16[256,896]{1,0:T(8,128)(2,1)}, u32[]{:S(2)}) copy-start(bf16[256,896]{1,0:T(8,128)(2,1)} %param.12) | copy-start | bytes 1376260
  146.6 25.3 %copy-start.4 = (bf16[64,8,128]{2,1,0:T(8,128)(2,1)S(1)}, bf16[64,8,128]{2,1,0:T(8,128)(2,1)}, u32[]{:S(2)}) copy-start(bf16[64,8,128]{2,1,0:T(8,128)(2,1)} %get-tuple-element.6) | copy-start | bytes 393220

commit v2 on v1

v2 whole, which is shorter than its diff:
```python
import math

import jax
import jax.numpy as jnp
import numpy as np
from jax import lax
from jax.experimental import pallas as pl
from jax.experimental.pallas import tpu as pltpu
from jax.sharding import Mesh
from jax.sharding import PartitionSpec as P

D = 3584
HEADS = 28
KV_HEADS = 4
HEAD_DIM = 128
RANK = 4
NX, NZ, NC, NY = 4, 8, 2, 4
PLANE = NX * NZ * NC
ROWS = D // PLANE
COLS = D // NY
AXES = ("pop_0", "pop_1", "pop_2", "mp")
POP = AXES[:3]
MESH = pl.DeviceIdType.MESH

noise_scale = 0.5
rope_base = 1000000.0
spread_floor = 0.001


def place():
    return tuple(lax.axis_index(a) for a in AXES)


def plane_device(p, y):
    return (p // (NZ * NC), (p // NC) % NZ, p % NC, y)


def meet_plane(me):
    x, z, c, y = me
    p = (x * NZ + z) * NC + c
    barrier = pltpu.get_barrier_semaphore()

    @pl.loop(1, PLANE)
    def _(i):
        pl.semaphore_signal(
            barrier, inc=1, device_id=plane_device((p + i) % PLANE, y), device_id_type=MESH
        )

    return barrier, PLANE - 1


def local_wait(ref, sem):
    pltpu.make_async_copy(ref, ref, sem).wait()


class PlaneGather:
    SEMS = 49

    def __init__(self, me, buf, sem, cut):
        self.x, self.z, self.c, self.y = me
        self.buf, self.sem = buf, sem
        self.a = pl.ds(0, cut)
        self.b = pl.ds(cut, COLS - cut)

    def zat(self, d):
        return (self.z + d + NZ) % NZ

    def yat(self, d):
        return (self.y + d + NY) % NY

    def send(self, ref, to, ssem, rsem):
        pltpu.make_async_remote_copy(
            src_ref=ref,
            dst_ref=ref,
            send_sem=self.sem.at[ssem],
            recv_sem=self.sem.at[rsem],
            device_id=to,
            device_id_type=MESH,
        ).start()

    def ydev(self, d):
        return (self.x, self.z, self.c, self.yat(d))

    def zdev(self, d):
        return (self.x, self.zat(d), self.c, self.y)

    def share(self, ref):
        self.send(ref, (self.x, self.z, 1 - self.c, self.y), 4, 5)

    def ra(self, right, s, h):
        return (7 if right else 15) + (s - 1) * 2 + h

    def rb(self, right, s):
        return (23 if right else 27) + s - 1

    def ry(self, right, k):
        return (31 if right else 39) + k

    @staticmethod
    def zoff(k):
        return -((k + 1) // 2) if k % 2 else k // 2

    def start(self):
        own_a = self.buf.at[self.y, self.z, self.c, :, self.a]
        own_b = self.buf.at[self.y, self.z, self.c, :, self.b]
        for d in (1, 3, 2):
            self.send(own_a, self.ydev(d), 0, 6)
        self.send(own_b, self.zdev(1), 2, self.rb(True, 1))
        self.send(own_b, self.zdev(-1), 2, self.rb(False, 1))
        self.send(own_b, self.ydev(1), 3, self.ry(True, 0))
        self.send(own_b, self.ydev(-1), 3, self.ry(False, 0))
        self.share(own_b)

    def a_line(self):
        local_wait(self.buf.at[pl.ds(0, 3), self.z, self.c, :, self.a], self.sem.at[6])
        for h in range(2):
            ref = self.buf.at[pl.ds(2 * h, 2), self.z, self.c, :, self.a]
            self.send(ref, self.zdev(1), 1, self.ra(True, 1, h))
            self.send(ref, self.zdev(-1), 1, self.ra(False, 1, h))
        self.share(self.buf.at[:, self.z, self.c, :, self.a])

    @staticmethod
    def a_moves(right, s, h):
        return s < 4 or (s == 4 and h == (0 if right else 1))

    def a_step(self, s):
        for h in range(2):
            for right in (True, False):
                if not self.a_moves(right, s, h):
                    continue
                zz = self.zat(-s if right else s)
                ref = self.buf.at[pl.ds(2 * h, 2), zz, self.c, :, self.a]
                local_wait(ref, self.sem.at[self.ra(right, s, h)])
                if s < 4 and self.a_moves(right, s + 1, h):
                    self.send(ref, self.zdev(1 if right else -1), 1, self.ra(right, s + 1, h))
                self.share(ref)

    def b_step(self, s):
        for right in (True, False):
            if s == 4 and not right:
                continue
            zz = self.zat(-s if right else s)
            k = 2 * s - 1 if right else 2 * s
            ref = self.buf.at[self.y, zz, self.c, :, self.b]
            local_wait(ref, self.sem.at[self.rb(right, s)])
            if s < 3 or (s == 3 and right):
                self.send(ref, self.zdev(1 if right else -1), 2, self.rb(right, s + 1))
            self.send(ref, self.ydev(1), 3, self.ry(True, k))
            self.send(ref, self.ydev(-1), 3, self.ry(False, k))
            self.share(ref)

    def y_step(self, k):
        zz = self.zat(self.zoff(k))
        for right in (True, False):
            ref = self.buf.at[self.yat(-1 if right else 1), zz, self.c, :, self.b]
            local_wait(ref, self.sem.at[self.ry(right, k)])
            if (k % 2 == 0) == right:
                self.send(ref, self.ydev(1 if right else -1), 3, 47 if right else 48)
            self.share(ref)

    def far(self):
        for s in (47, 48):
            local_wait(self.buf.at[0, pl.ds(0, 4), self.c, :, self.b], self.sem.at[s])
        self.share(self.buf.at[self.yat(2), :, self.c, :, self.b])

    def finish(self):
        local_wait(self.buf.at[:, :, 1 - self.c], self.sem.at[5])

    def drain(self):
        local_wait(self.buf.at[pl.ds(0, 3), 0, 0, :, self.a], self.sem.at[0])
        local_wait(self.buf.at[:, pl.ds(0, 7), 0, :, self.a], self.sem.at[1])
        local_wait(self.buf.at[0, pl.ds(0, 7), 0, :, self.b], self.sem.at[2])
        local_wait(self.buf.at[pl.ds(0, 3), :, 0, :, self.b], self.sem.at[3])
        local_wait(self.buf.at[:, :, self.c], self.sem.at[4])


CUT = 256
SLAB = 16
FAR_FIRST = (1, 7, 2, 6, 3, 5, 4)


def remote(src, dst, ssem, rsem, to):
    pltpu.make_async_remote_copy(
        src_ref=src, dst_ref=dst, send_sem=ssem, recv_sem=rsem, device_id=to, device_id_type=MESH
    ).start()


def forward_kernel(
    tok_h, wk_h, wv_h, wo_h, tgt_h, s_h, fac_h, lft_h, cos_h, sin_h,
    ev, fac_all, s_out,
    tok, wk, wv, tgt, s_in, fac, lft, cos, sin,
    wbuf, bt, mt, k4, v4, fb, lft_m, tgt_m, tgt_t, acc, low, part, total,
    sem_l, sem_w, sem_s, sem_t, sem_k, sem_1, sem_2, sem_3, sem_4, sem_f, sem_e,
):
    me = place()
    x, z, c, y = me
    p = (x * NZ + z) * NC + c
    f32, bf16 = jnp.float32, jnp.bfloat16
    tokens_n = tok.shape[0]
    half = HEAD_DIM // 2

    loads = {}
    for i, (name, src, dst) in enumerate(
        (
            ("wo", wo_h, wbuf.at[y, z, c]),
            ("s", s_h, s_in),
            ("lft", lft_h, lft),
            ("fac", fac_h, fac),
            ("own", fac_h, fac_all.at[x * NZ + z, c]),
            ("tgt", tgt_h, tgt),
            ("tok", tok_h, tok),
            ("wk", wk_h, wk),
            ("wv", wv_h, wv),
            ("cos", cos_h, cos),
            ("sin", sin_h, sin),
        )
    ):
        loads[name] = pltpu.make_async_copy(src, dst, sem_l.at[i])
        loads[name].start()

    barrier = pltpu.get_barrier_semaphore()

    def greet(to):
        pl.semaphore_signal(barrier, inc=1, device_id=to, device_id_type=MESH)

    @pl.loop(1, PLANE)
    def _(i):
        greet(plane_device((p + i) % PLANE, y))

    @pl.loop(0, 3 * NZ * NC)
    def _(i):
        greet((x, (i // NC) % NZ, i % NC, (y + 1 + i // (NZ * NC)) % NY))

    for dx in range(1, NX):
        for dy in range(1, NY):
            greet(((x + dx) % NX, z, c, (y + dy) % NY))

    fb[:, :, pl.ds(COLS, 128)] = jnp.zeros((NY, 8, 128), bf16)
    pl.semaphore_wait(barrier, PLANE - 1 + 3 * NZ * NC + 9)

    wide = PlaneGather(me, wbuf, sem_w, CUT)
    loads["s"].wait()

    @pl.loop(1, PLANE)
    def _(i):
        to = (p + i) % PLANE
        remote(s_in.at[to], s_out.at[p], sem_s.at[0], sem_s.at[1], plane_device(to, y))

    for name in ("lft", "fac", "tgt"):
        loads[name].wait()

    @pl.when(x != y)
    def _():
        remote(lft, lft_m, sem_t.at[0], sem_t.at[1], (y, z, c, x))
        remote(fac, fb.at[y, :, pl.ds(0, COLS)], sem_t.at[4], sem_t.at[5], (x, z, c, x))
        remote(tgt, tgt_m, sem_t.at[2], sem_t.at[3], (y, z, c, x))

    for d in range(1, NX):
        remote(fac, fb.at[y, :, pl.ds(0, COLS)], sem_t.at[4], sem_t.at[5], ((x + d) % NX, z, c, x))

    @pl.when(x == y)
    def _():
        lft_m[...] = lft[...]
        fb[y, :, pl.ds(0, COLS)] = fac[...]
        tgt_m[...] = tgt[...]

    loads["wo"].wait()
    wide.start()
    s_out[p] = s_in[p]

    for name in ("tok", "wk", "wv", "cos", "sin"):
        loads[name].wait()

    def turned(v):
        first, second = v[:half], v[half:]
        ct, st = cos[...], sin[...]
        return jnp.concatenate([first * ct - second * st, second * ct + first * st], axis=0)

    key_t = jnp.dot(tok[...], wk[...], preferred_element_type=f32).T
    k4[y] = turned(key_t).T.astype(bf16)
    v4[y] = jnp.dot(tok[...], wv[...], preferred_element_type=f32).T.astype(bf16)
    for d in range(1, NY):
        to = (x, z, c, (y + d) % NY)
        remote(k4.at[y], k4.at[y], sem_k.at[0], sem_k.at[1], to)
        remote(v4.at[y], v4.at[y], sem_k.at[2], sem_k.at[3], to)

    wide.a_line()

    @pl.when(x != y)
    def _():
        local_wait(lft_m, sem_t.at[1])

    local_wait(s_out.at[pl.ds(0, PLANE - 1)], sem_s.at[1])
    slab = jnp.concatenate([s_out[i, pl.ds(0, SLAB), pl.ds(0, ROWS)] for i in range(PLANE)], axis=1)
    made = lax.dot_general(
        jnp.concatenate([slab, lft_m[...]], axis=0),
        tok[...],
        (((1,), (1,)), ((), ())),
        preferred_element_type=f32,
    )
    bt[y, x, z, c] = made[:SLAB].astype(bf16)
    low[...] = made[SLAB : SLAB + 8].astype(bf16)
    for d in range(1, NY):
        own = bt.at[y, x, z, c]
        remote(own, own, sem_1.at[0], sem_1.at[1], (x, z, c, (y + d) % NY))

    wide.b_step(1)
    wide.y_step(0)

    @pl.when(x != y)
    def _():
        local_wait(tgt_m, sem_t.at[3])

    tgt_t[...] = tgt_m[...].astype(f32).T

    local_wait(bt.at[pl.ds(0, 3), 0, 0, 0], sem_1.at[1])

    def line_out(zz):
        ref = bt.at[:, x, zz, c]
        for d in (1, 3, 2):
            remote(ref, ref, sem_3.at[0], sem_3.at[d], ((x + d) % NX, z, c, y))
        remote(ref, ref, sem_4.at[0], sem_4.at[1], (x, z, 1 - c, y))

    mine = bt.at[:, x, z, c]
    for d in FAR_FIRST:
        remote(mine, mine, sem_2.at[0], sem_2.at[d], (x, (z + d) % NZ, c, y))
    line_out(z)

    def line_in(d):
        zz = (z + NZ - d) % NZ
        local_wait(bt.at[:, x, zz, c], sem_2.at[d])
        line_out(zz)

    wide.a_step(1)
    for d in FAR_FIRST[:3]:
        line_in(d)
    wide.b_step(2)
    wide.y_step(1)
    wide.y_step(2)
    for d in FAR_FIRST[3:]:
        line_in(d)
    wide.a_step(2)

    row = lax.broadcasted_iota(jnp.int32, (tokens_n, tokens_n), 0)
    col = lax.broadcasted_iota(jnp.int32, (tokens_n, tokens_n), 1)

    def attend(xb):
        @pl.loop(0, NY)
        def _(yh):
            right = fb[yh, pl.ds(0, RANK), pl.ds(pl.multiple_of(xb * 256, 256), 256)]
            shift = lax.dot_general(
                right, low[pl.ds(0, RANK), :], (((0,), (0,)), ((), ())), preferred_element_type=f32
            )
            base = bt[yh, xb].reshape(2 * HEAD_DIM, tokens_n).astype(f32)
            query = base + noise_scale * shift
            for j in range(2):
                q = turned(query[j * HEAD_DIM : (j + 1) * HEAD_DIM]).astype(bf16)
                scores = jnp.dot(k4[yh], q, preferred_element_type=f32) * HEAD_DIM ** (-0.5)
                scores = jnp.where(row <= col, scores, -1e30)
                scores = jnp.exp(scores - jnp.max(scores, axis=0, keepdims=True))
                probs = scores / jnp.sum(scores, axis=0, keepdims=True)
                mixed = jnp.dot(v4[yh], probs.astype(bf16), preferred_element_type=f32)
                mt[yh, xb * 2 + j] = mixed.astype(bf16)

    local_wait(bt.at[:, x, :, 1 - c], sem_4.at[1])
    for k in (1, 3):
        local_wait(k4.at[pl.ds(0, 3)] if k == 1 else v4.at[pl.ds(0, 3)], sem_k.at[k])

    @pl.when(x != y)
    def _():
        local_wait(fb.at[:, :, pl.ds(0, COLS)], sem_t.at[5])

    @pl.when(x == y)
    def _():
        local_wait(fb.at[pl.ds(0, 3), :, pl.ds(0, COLS)], sem_t.at[5])

    attend(x)
    wide.b_step(3)
    wide.y_step(3)
    wide.y_step(4)
    wide.a_step(3)

    def block_in(d):
        ref = bt.at[:, (x + NX - d) % NX, :, c]
        local_wait(ref, sem_3.at[d])
        remote(ref, ref, sem_4.at[0], sem_4.at[1 + d], (x, z, 1 - c, y))

    def block_use(d):
        xb = (x + NX - d) % NX
        local_wait(bt.at[:, xb, :, 1 - c], sem_4.at[1 + d])
        attend(xb)

    block_in(1)
    block_in(3)
    wide.b_step(4)
    wide.y_step(5)
    wide.y_step(6)
    wide.a_step(4)
    block_in(2)
    wide.y_step(7)
    wide.far()
    chip = x * NZ + z
    own = fac_all.at[chip, c]
    loads["own"].wait()

    @pl.loop(1, NX * NZ)
    def _(i):
        to = (chip + i) % (NX * NZ)
        remote(own, own, sem_f.at[0], sem_f.at[1], (to // NZ, to % NZ, c, y))

    block_use(1)
    block_use(3)
    block_use(2)

    wide.finish()
    out_right = lft_m[pl.ds(RANK, RANK), pl.ds(pl.multiple_of(x * COLS, 128), COLS)].astype(f32)
    acc[...] = -tgt_t[...]

    @pl.loop(0, NY)
    def _(b):
        rows = mt[b, pl.ds(0, 7)].reshape(COLS, tokens_n)
        term = jnp.dot(wbuf[b].reshape(COLS, COLS), rows, preferred_element_type=f32)
        low_o = jnp.dot(fb[b, pl.ds(RANK, RANK), pl.ds(0, COLS)], rows, preferred_element_type=f32)
        shift = lax.dot_general(
            out_right,
            low_o,
            (((0,), (0,)), ((), ())),
            precision=lax.Precision.HIGHEST,
            preferred_element_type=f32,
        )
        acc[...] += (term + noise_scale * shift).astype(bf16).astype(f32)

    part[x] = jnp.full((1, 128), jnp.sum(acc[...] * acc[...]), f32)
    for d in range(1, NX):
        remote(part.at[x], part.at[x], sem_e.at[0], sem_e.at[1], ((x + d) % NX, z, c, y))
    local_wait(fac_all.at[pl.ds(0, NX * NZ - 1), c], sem_f.at[1])
    remote(fac_all.at[:, c], fac_all.at[:, c], sem_f.at[2], sem_f.at[3], (x, z, 1 - c, y))
    local_wait(part.at[pl.ds(0, NX - 1)], sem_e.at[1])
    total[...] = part[0] + part[1] + part[2] + part[3]
    slot = (y * NZ + z) * NC + c
    ev[slot] = total[...]

    @pl.loop(1, PLANE)
    def _(i):
        to = (slot + i) % PLANE
        remote(
            total,
            ev.at[slot],
            sem_e.at[2],
            sem_e.at[3],
            (x, (to // NC) % NZ, to % NC, to // (NZ * NC)),
        )

    local_wait(ev.at[pl.ds(0, PLANE - 1)], sem_e.at[3])
    local_wait(fac_all.at[:, 1 - c], sem_f.at[3])

    wide.drain()
    local_wait(s_out.at[pl.ds(0, PLANE - 1)], sem_s.at[0])

    @pl.when(x != y)
    def _():
        local_wait(lft_m, sem_t.at[0])
        local_wait(tgt_m, sem_t.at[2])
        local_wait(fb.at[:, :, pl.ds(0, COLS)], sem_t.at[4])

    @pl.when(x == y)
    def _():
        local_wait(fb.at[pl.ds(0, 3), :, pl.ds(0, COLS)], sem_t.at[4])

    local_wait(k4.at[pl.ds(0, 3)], sem_k.at[0])
    local_wait(v4.at[pl.ds(0, 3)], sem_k.at[2])
    local_wait(bt.at[pl.ds(0, 3), 0, 0, 0], sem_1.at[0])
    local_wait(bt.at[:, 0, pl.ds(0, 7), 0], sem_2.at[0])
    local_wait(bt.at[:, pl.ds(0, 3), :, 0], sem_3.at[0])
    local_wait(bt.at[:, :, :, 0], sem_4.at[0])
    local_wait(fac_all.at[pl.ds(0, NX * NZ - 1), c], sem_f.at[0])
    local_wait(fac_all.at[:, c], sem_f.at[2])
    local_wait(part.at[pl.ds(0, NX - 1)], sem_e.at[0])
    local_wait(ev.at[pl.ds(0, PLANE - 1)], sem_e.at[2])


def forward(tokens, w_key, w_value, wo_t, target, s_in, fac, lft, cos_t, sin_t):
    tok = tokens.shape[0]
    bf16, f32 = jnp.bfloat16, jnp.float32
    ins = (tokens, w_key, w_value, wo_t, target, s_in, fac, lft, cos_t, sin_t)
    held = (tokens, w_key, w_value, target, s_in, fac, lft, cos_t, sin_t)
    dma = pltpu.SemaphoreType.DMA
    return pl.pallas_call(
        forward_kernel,
        name="forward",
        out_shape=(
            jax.ShapeDtypeStruct((PLANE, 1, 128), f32),
            jax.ShapeDtypeStruct((NX * NZ, NC, 8, COLS), bf16),
            jax.ShapeDtypeStruct(s_in.shape, bf16),
        ),
        in_specs=[pl.BlockSpec(memory_space=pl.ANY)] * len(ins),
        out_specs=[pl.BlockSpec(memory_space=pltpu.VMEM)] * 3,
        scratch_shapes=[pltpu.VMEM(a.shape, a.dtype) for a in held]
        + [
            pltpu.VMEM((NY, NZ, NC, ROWS, COLS), bf16),
            pltpu.VMEM((NY, NX, NZ, NC, SLAB, tok), bf16),
            pltpu.VMEM((NY, 8, HEAD_DIM, tok), bf16),
            pltpu.VMEM((NY, tok, HEAD_DIM), bf16),
            pltpu.VMEM((NY, HEAD_DIM, tok), bf16),
            pltpu.VMEM((NY, 8, COLS + 128), bf16),
            pltpu.VMEM((8, D), bf16),
            pltpu.VMEM((tok, COLS), bf16),
            pltpu.VMEM((COLS, tok), f32),
            pltpu.VMEM((COLS, tok), f32),
            pltpu.VMEM((8, tok), bf16),
            pltpu.VMEM((NX, 1, 128), f32),
            pltpu.VMEM((1, 128), f32),
            dma((11,)),
            dma((PlaneGather.SEMS,)),
            dma((2,)),
            dma((6,)),
            dma((4,)),
            dma((2,)),
            dma((8,)),
            dma((4,)),
            dma((5,)),
            dma((4,)),
            dma((4,)),
        ],
        compiler_params=pltpu.CompilerParams(
            collective_id=0, has_side_effects=True, vmem_limit_bytes=60 * 1024 * 1024
        ),
    )(*ins)


def tables(count, head_size):
    position = np.arange(count, dtype=np.float64)
    index = np.arange(head_size // 2, dtype=np.float64)
    freq = np.exp(-math.log(rope_base) * 2.0 * index / head_size)
    angle = freq[:, None] * position[None, :]
    return np.cos(angle).astype(np.float32), np.sin(angle).astype(np.float32)


def per_device(
    tokens,
    target,
    w_query,
    w_key,
    w_value,
    w_out,
    query_left_factors,
    query_right_factors,
    o_left,
    o_right,
    member_ids,
):
    tok = tokens.shape[0]
    f32, bf16 = jnp.float32, jnp.bfloat16
    cos_t, sin_t = tables(tok, HEAD_DIM)
    signs = (1 - 2 * (member_ids % 2)).astype(bf16)
    lft = jnp.concatenate([jnp.transpose(query_left_factors[0]), o_right[0]], axis=0) * signs
    fac = jnp.concatenate([query_right_factors[0], jnp.transpose(o_left[0])], axis=0)
    slabs = jnp.transpose(w_query).reshape(COLS // SLAB, SLAB, ROWS)
    slabs = jnp.pad(slabs, ((0, PLANE - COLS // SLAB), (0, 0), (0, 128 - ROWS)))
    lefts = jnp.transpose(lft.reshape(2 * RANK, PLANE, ROWS), (1, 0, 2))
    lefts = jnp.pad(lefts, ((0, 0), (0, 0), (0, 128 - ROWS)))
    s_in = jnp.concatenate([slabs, lefts], axis=1)
    errors, facs, s_out = forward(
        tokens, w_key, w_value, jnp.transpose(w_out), target, s_in, fac, lft, cos_t, sin_t
    )
    everyone = -(errors[:, 0, 0] / (tok * D))
    p = (lax.axis_index(POP[0]) * NZ + lax.axis_index(POP[1])) * NC + lax.axis_index(POP[2])
    fitness = lax.dynamic_slice(everyone, (p,), (1,))
    mean = jnp.sum(everyone) / PLANE
    spread = jnp.sum((everyone - mean) * (everyone - mean)) / PLANE
    unsigned = (everyone - mean) / jnp.sqrt(spread + spread_floor)
    lefts = s_out[:, SLAB:, :ROWS].astype(f32) * unsigned[:, None, None]
    rights = facs.reshape(PLANE, 2 * RANK, COLS).astype(f32)

    def gradient(left, right):
        return (
            lax.dot_general(
                left.reshape(-1, ROWS),
                right.reshape(-1, COLS),
                (((0,), (0,)), ((), ())),
                precision=lax.Precision.HIGHEST,
            )
            / noise_scale
        )

    grad_query = gradient(lefts[:, :RANK], rights[:, :RANK])
    grad_out = gradient(lefts[:, RANK:], rights[:, RANK:])
    return (grad_query, jnp.transpose(grad_out), fitness)


def solution(mesh):
    torus = Mesh(mesh.devices.reshape(NX, NZ, NC, NY), AXES)
    placed = (
        P(),
        P(None, "mp"),
        P(POP, "mp"),
        P(None, "mp"),
        P(None, "mp"),
        P("mp", POP),
        P(POP, None, None),
        P(POP, None, "mp"),
        P(POP, "mp", None),
        P(POP, None, None),
        P(POP),
    )
    return jax.shard_map(
        per_device,
        mesh=torus,
        in_specs=placed,
        out_specs=(P(POP, "mp"), P("mp", POP), P(POP)),
        check_vma=False,
    )
```

time: 177 us -> 122 us (0.69)
  matrix products: 26.4 us -> 2.12 us
  Pallas kernels: 118 us -> 105 us
  local copies, waits for them, and re-layouts: 17 us -> 5.33 us
  other arithmetic: 11.8 us -> 6.67 us
    dot_general x7 -> x0, matrix products: 21.1 us -> none  [the longest x1 6.52 us: per_device(): jnp.dot(wide.reshape(tok, -1), g1.reshape(-1, COLS), preferred_element_ty...]
    pallas_call x3 -> x1, Pallas kernels: 118 us -> 105 us  [forward(): pl.pallas_call(forward_kernel, name='forward', out_shape=(jax.ShapeDtypeS...]
    unnamed x22 -> x8, local copies, waits for them, and re-layouts: 6.83 us -> 0.02 us
    sub x1 -> x0, matrix products: 3.12 us -> none  [per_device(): probs = jax.nn.softmax(scores, axis=-1).astype(jnp.bfloat16)]
    reduce_sum x2 -> x0, other arithmetic: 2.73 us -> none  [the longest x1 1.89 us: per_device(): output = jnp.sum(arrived.astype(f32), axis=0)]
    another operation x1 -> x0, other arithmetic: 2.51 us -> none
    add x1 -> x0, local copies, waits for them, and re-layouts: 2.42 us -> none  [per_device(): base + factor * jnp.dot(low_q, query_right_factors[0], preferred_element_...]
    slice x1 -> x0, local copies, waits for them, and re-layouts: 2.01 us -> none  [rotate(): second = field[..., half:]]
where the time goes in v2:
time: 122 us; the launch traced here: 121 us
  Pallas kernels  105 us (86%)
  other arithmetic  6.67 us (5%)
  local copies, waits for them, and re-layouts  5.33 us (4%)
  between operations  2.78 us (2%)
  matrix products  2.12 us (2%)
    pallas_call x1, Pallas kernels, forward(): pl.pallas_call(forward_kernel, name='forward', out_shape=(jax.ShapeDtypeS...  105 us

profile of v2, /device:TPU:1, one launch (start us, length us, event | category | flops | bytes accessed | tf_op | source)
XLA Modules:
  0.0 121.4 jit_solution(17301643799731470002)
XLA Ops:
  0.6 0.0 copy-start.1
  0.6 0.0 copy-start
  0.7 0.0 copy-start.3
  0.7 0.0 copy-start.2
  1.4 0.9 concatenate.16
  2.3 0.1 copy.23
  2.3 0.9 concatenate.17
  3.2 0.1 copy.24
  3.3 0.1 fusion.7
  3.4 1.1 copy.22
  4.5 0.8 fusion.6.s_h
  5.3 0.0 copy-done.1
  5.3 0.0 copy-done
  5.3 0.7 maximum_multiply_fusion.1.lft_h
  6.0 0.0 copy-done.3
  6.0 0.0 copy-done.2
  6.0 0.6 pad_maximum_fusion.fac_h
  6.6 104.5 %forward.1 = (f32[64,1,128]{2,1,0:T(1,128)}, bf16[32,2,8,896]{3,2,1,0:T(8,128)(2,1)}, bf16[64,24,128]{2,1,0:T(8,128)(2,1)}) custom-call(bf16[256,3584]{1,0:T(8,128)(2,1)} %tok_h.1, bf16[3584,128]{1,0:T(8,128)(2,1)} %wk_h.1, bf16[3584,128]{1,0:T(8,128)(2,1)} %wv_h.1, bf16[56,896]{1,0:T(8,128)(2,1)} %bitcast.30, bf16[256,896]{1,0:T(8,128)(2,1)} %tgt_h.1, ...), custom_call_target="tpu_custom_call" | custom-call | tf_op jit(solution)/shard_map/forward/pallas_call | solution.py:488
  111.1 1.4 %fusion.10 = f32[]{:T(128)} fusion(f32[64,1,128]{2,1,0:T(1,128)} %get-tuple-element.7), kind=kLoop, calls=%fused_computation.21 | loop fusion | flops 127 | bytes 260 | tf_op jit(solution)/shard_map/reduce_sum | solution.py:569
  113.2 1.4 %multiply_reduce_fusion = (f32[]{:T(128)}, f32[64,1,1]{2,1,0:T(1,128)S(1)}) fusion(f32[]{:T(128)S(6)} %div.27, f32[64,1,128]{2,1,0:T(1,128)} %get-tuple-element.7), kind=kLoop, calls=%fused_computation.17 | loop fusion | flops 319 | bytes 520 | tf_op jit(solution)/shard_map/reduce_sum | solution.py:570
  115.3 0.6 divide_reduce_fusion
  115.9 1.0 convert_multiply_fusion
  117.0 1.8 %fusion.13 = (bf16[64,4,896]{2,1,0:T(4,128)(2,1)S(1)}, bf16[64,4,896]{2,1,0:T(4,128)(2,1)S(1)}) fusion(bf16[64,8,896]{2,1,0:T(8,128)(2,1)} %bitcast.24), kind=kLoop, calls=%fused_computation.24 | loop fusion | bytes 1835008 | tf_op jit(solution)/shard_map/slice | solution.py:587
  118.8 1.1 fusion
  119.8 1.1 fusion.1
  120.9 0.5 constant_dynamic-slice_fusion
  (1 shorter events, 0.0 us)
Async XLA Ops:
  0.6 4.7 %copy-start.1 = (bf16[1,3584,4]{1,2,0:T(4,128)(2,1)S(1)}, bf16[1,3584,4]{1,2,0:T(4,128)(2,1)}, u32[]{:S(2)}) copy-start(bf16[1,3584,4]{1,2,0:T(4,128)(2,1)} %param.19) | copy-start | bytes 86020
  0.6 4.7 %copy-start = (bf16[1,4,3584]{2,1,0:T(4,128)(2,1)S(1)}, bf16[1,4,3584]{2,1,0:T(4,128)(2,1)}, u32[]{:S(2)}) copy-start(bf16[1,4,3584]{2,1,0:T(4,128)(2,1)} %param.22) | copy-start | bytes 86020
  0.7 5.3 %copy-start.3 = (bf16[1,4,896]{2,1,0:T(4,128)(2,1)S(1)}, bf16[1,4,896]{2,1,0:T(4,128)(2,1)}, u32[]{:S(2)}) copy-start(bf16[1,4,896]{2,1,0:T(4,128)(2,1)} %param.20) | copy-start | bytes 21508
  0.7 5.3 %copy-start.2 = (bf16[1,896,4]{1,2,0:T(4,128)(2,1)S(1)}, bf16[1,896,4]{1,2,0:T(4,128)(2,1)}, u32[]{:S(2)}) copy-start(bf16[1,896,4]{1,2,0:T(4,128)(2,1)} %param.21) | copy-start | bytes 21508

commit v3 on v2

--- a/solution.py
+++ b/solution.py
@@ -35,20 +35,6 @@
     return (p // (NZ * NC), (p // NC) % NZ, p % NC, y)
 
 
-def meet_plane(me):
-    x, z, c, y = me
-    p = (x * NZ + z) * NC + c
-    barrier = pltpu.get_barrier_semaphore()
-
-    @pl.loop(1, PLANE)
-    def _(i):
-        pl.semaphore_signal(
-            barrier, inc=1, device_id=plane_device((p + i) % PLANE, y), device_id_type=MESH
-        )
-
-    return barrier, PLANE - 1
-
-
 def local_wait(ref, sem):
     pltpu.make_async_copy(ref, ref, sem).wait()
 
@@ -58,7 +44,8 @@
 
     def __init__(self, me, buf, sem, cut):
         self.x, self.z, self.c, self.y = me
-        self.buf, self.sem = buf, sem
+        self.sem = sem
+        self.buf = buf
         self.a = pl.ds(0, cut)
         self.b = pl.ds(cut, COLS - cut)
 
@@ -164,14 +151,14 @@
         self.share(self.buf.at[self.yat(2), :, self.c, :, self.b])
 
     def finish(self):
-        local_wait(self.buf.at[:, :, 1 - self.c], self.sem.at[5])
+        local_wait(self.buf.at[:, :, 1 - self.c, :, pl.ds(0, COLS)], self.sem.at[5])
 
     def drain(self):
         local_wait(self.buf.at[pl.ds(0, 3), 0, 0, :, self.a], self.sem.at[0])
         local_wait(self.buf.at[:, pl.ds(0, 7), 0, :, self.a], self.sem.at[1])
         local_wait(self.buf.at[0, pl.ds(0, 7), 0, :, self.b], self.sem.at[2])
         local_wait(self.buf.at[pl.ds(0, 3), :, 0, :, self.b], self.sem.at[3])
-        local_wait(self.buf.at[:, :, self.c], self.sem.at[4])
+        local_wait(self.buf.at[:, :, self.c, :, pl.ds(0, COLS)], self.sem.at[4])
 
 
 CUT = 256
@@ -186,11 +173,12 @@
 
 
 def forward_kernel(
-    tok_h, wk_h, wv_h, wo_h, tgt_h, s_h, fac_h, lft_h, cos_h, sin_h,
-    ev, fac_all, s_out,
-    tok, wk, wv, tgt, s_in, fac, lft, cos, sin,
-    wbuf, bt, mt, k4, v4, fb, lft_m, tgt_m, tgt_t, acc, low, part, total,
-    sem_l, sem_w, sem_s, sem_t, sem_k, sem_1, sem_2, sem_3, sem_4, sem_f, sem_e,
+    ids, tok_h, wk_h, wv_h, wo_h, tgt_h, wq_h, ql_h, qr_h, ol_h, or_h, cos_h, sin_h,
+    grad_q, grad_o, fit,
+    tok, wk, wv, tgt, wq, ql, qr, ol, orr, cos, sin,
+    slab_in, slab_out, left_in, left_out, fac, fac_all, lft, ev,
+    wbuf, bt, mt, k4, v4, fb, lft_m, tgt_t, acc, low, part, total,
+    sem_l, sem_w, sem_s, sem_t, sem_k, sem_1, sem_2, sem_3, sem_4, sem_f, sem_e, sem_g,
 ):
     me = place()
     x, z, c, y = me
@@ -198,21 +186,23 @@
     f32, bf16 = jnp.float32, jnp.bfloat16
     tokens_n = tok.shape[0]
     half = HEAD_DIM // 2
+    sibling = (x, z, 1 - c, y)
 
     loads = {}
     for i, (name, src, dst) in enumerate(
         (
-            ("wo", wo_h, wbuf.at[y, z, c]),
-            ("s", s_h, s_in),
-            ("lft", lft_h, lft),
-            ("fac", fac_h, fac),
-            ("own", fac_h, fac_all.at[x * NZ + z, c]),
-            ("tgt", tgt_h, tgt),
+            ("wq", wq_h, wq),
+            ("ql", ql_h, ql),
+            ("or", or_h, orr),
+            ("qr", qr_h, qr),
+            ("ol", ol_h, ol),
+            ("wo", wo_h, wbuf.at[y, z, c, :, pl.ds(0, COLS)]),
             ("tok", tok_h, tok),
             ("wk", wk_h, wk),
             ("wv", wv_h, wv),
             ("cos", cos_h, cos),
             ("sin", sin_h, sin),
+            ("tgt", tgt_h, tgt),
         )
     ):
         loads[name] = pltpu.make_async_copy(src, dst, sem_l.at[i])
@@ -235,54 +225,60 @@
         for dy in range(1, NY):
             greet(((x + dx) % NX, z, c, (y + dy) % NY))
 
-    fb[:, :, pl.ds(COLS, 128)] = jnp.zeros((NY, 8, 128), bf16)
-    pl.semaphore_wait(barrier, PLANE - 1 + 3 * NZ * NC + 9)
-
-    wide = PlaneGather(me, wbuf, sem_w, CUT)
-    loads["s"].wait()
-
-    @pl.loop(1, PLANE)
-    def _(i):
-        to = (p + i) % PLANE
-        remote(s_in.at[to], s_out.at[p], sem_s.at[0], sem_s.at[1], plane_device(to, y))
-
-    for name in ("lft", "fac", "tgt"):
-        loads[name].wait()
-
-    @pl.when(x != y)
-    def _():
-        remote(lft, lft_m, sem_t.at[0], sem_t.at[1], (y, z, c, x))
-        remote(fac, fb.at[y, :, pl.ds(0, COLS)], sem_t.at[4], sem_t.at[5], (x, z, c, x))
-        remote(tgt, tgt_m, sem_t.at[2], sem_t.at[3], (y, z, c, x))
-
-    for d in range(1, NX):
-        remote(fac, fb.at[y, :, pl.ds(0, COLS)], sem_t.at[4], sem_t.at[5], ((x + d) % NX, z, c, x))
-
-    @pl.when(x == y)
-    def _():
-        lft_m[...] = lft[...]
-        fb[y, :, pl.ds(0, COLS)] = fac[...]
-        tgt_m[...] = tgt[...]
-
-    loads["wo"].wait()
-    wide.start()
-    s_out[p] = s_in[p]
-
-    for name in ("tok", "wk", "wv", "cos", "sin"):
-        loads[name].wait()
-
     def turned(v):
         first, second = v[:half], v[half:]
         ct, st = cos[...], sin[...]
         return jnp.concatenate([first * ct - second * st, second * ct + first * st], axis=0)
 
+    sign = (1 - 2 * (ids[0] % 2)).astype(f32)
+    for name in ("wq", "ql", "or", "qr", "ol"):
+        loads[name].wait()
+    slab_in[pl.ds(0, COLS // SLAB), :, pl.ds(0, ROWS)] = (
+        wq[...].astype(f32).T.reshape(COLS // SLAB, SLAB, ROWS).astype(bf16)
+    )
+    slab_in[pl.ds(COLS // SLAB, PLANE - COLS // SLAB)] = jnp.zeros(
+        (PLANE - COLS // SLAB, SLAB, 128), bf16
+    )
+    fac[...] = jnp.concatenate([qr[...].astype(f32), ol[...].astype(f32)], axis=0).astype(bf16)
+    lft[...] = (jnp.concatenate([ql[...].astype(f32), orr[...].astype(f32)], axis=0) * sign).astype(bf16)
+    for i in range(PLANE):
+        left_in[i, :, pl.ds(0, ROWS)] = lft[:, pl.ds(i * ROWS, ROWS)]
+    fb[:, :, pl.ds(COLS, 128)] = jnp.zeros((NY, 8, 128), bf16)
+    slab_out[p] = slab_in[p]
+    left_out[p] = left_in[p]
+    fac_all[x * NZ + z, c] = fac[...]
+
+    for name in ("tok", "wk", "wv", "cos", "sin"):
+        loads[name].wait()
     key_t = jnp.dot(tok[...], wk[...], preferred_element_type=f32).T
     k4[y] = turned(key_t).T.astype(bf16)
     v4[y] = jnp.dot(tok[...], wv[...], preferred_element_type=f32).T.astype(bf16)
+    loads["wo"].wait()
+    loads["tgt"].wait()
+    pl.semaphore_wait(barrier, PLANE - 1 + 3 * NZ * NC + 9)
+
+    @pl.loop(1, PLANE)
+    def _(i):
+        to = (p + i) % PLANE
+        remote(slab_in.at[to], slab_out.at[p], sem_s.at[0], sem_s.at[1], plane_device(to, y))
+
+    @pl.when(x != y)
+    def _():
+        remote(lft, lft_m, sem_t.at[0], sem_t.at[1], (y, z, c, x))
+
+    wide = PlaneGather(me, wbuf, sem_w, CUT)
+    wide.start()
+
+    key_half = k4.at[y, pl.ds(pl.multiple_of(c * 128, 128), 128)]
+    value_half = v4.at[y, pl.ds(pl.multiple_of(c * 64, 64), 64)]
     for d in range(1, NY):
         to = (x, z, c, (y + d) % NY)
-        remote(k4.at[y], k4.at[y], sem_k.at[0], sem_k.at[1], to)
-        remote(v4.at[y], v4.at[y], sem_k.at[2], sem_k.at[3], to)
+        remote(key_half, key_half, sem_k.at[0], sem_k.at[1], to)
+        remote(value_half, value_half, sem_k.at[2], sem_k.at[3], to)
+
+    @pl.when(x == y)
+    def _():
+        lft_m[...] = lft[...]
 
     wide.a_line()
 
@@ -290,8 +286,8 @@
     def _():
         local_wait(lft_m, sem_t.at[1])
 
-    local_wait(s_out.at[pl.ds(0, PLANE - 1)], sem_s.at[1])
-    slab = jnp.concatenate([s_out[i, pl.ds(0, SLAB), pl.ds(0, ROWS)] for i in range(PLANE)], axis=1)
+    local_wait(slab_out.at[pl.ds(0, PLANE - 1)], sem_s.at[1])
+    slab = jnp.concatenate([slab_out[i, :, pl.ds(0, ROWS)] for i in range(PLANE)], axis=1)
     made = lax.dot_general(
         jnp.concatenate([slab, lft_m[...]], axis=0),
         tok[...],
@@ -304,14 +300,29 @@
         own = bt.at[y, x, z, c]
         remote(own, own, sem_1.at[0], sem_1.at[1], (x, z, c, (y + d) % NY))
 
+    tgt_half = tgt.at[pl.ds(pl.multiple_of(c * 128, 128), 128)]
+
+    @pl.when(x == y)
+    def _():
+        for d in range(1, NY):
+            to = (x, z, c, (y + d) % NY)
+            remote(tgt_half, tgt_half, sem_t.at[2], sem_t.at[3], to)
+
+    spot = fb.at[y, :, pl.ds(0, COLS)]
+
+    @pl.when(x != y)
+    def _():
+        remote(fac, spot, sem_t.at[4], sem_t.at[5], (x, z, c, x))
+
+    for d in range(1, NX):
+        remote(fac, spot, sem_t.at[4], sem_t.at[5], ((x + d) % NX, z, c, x))
+
+    @pl.when(x == y)
+    def _():
+        fb[y, :, pl.ds(0, COLS)] = fac[...]
+
     wide.b_step(1)
     wide.y_step(0)
-
-    @pl.when(x != y)
-    def _():
-        local_wait(tgt_m, sem_t.at[3])
-
-    tgt_t[...] = tgt_m[...].astype(f32).T
 
     local_wait(bt.at[pl.ds(0, 3), 0, 0, 0], sem_1.at[1])
 
@@ -341,8 +352,22 @@
         line_in(d)
     wide.a_step(2)
 
+    local_wait(k4.at[pl.ds(0, 3), pl.ds(0, 128)], sem_k.at[1])
+    keys_in = k4.at[:, pl.ds(pl.multiple_of(c * 128, 128), 128)]
+    remote(keys_in, keys_in, sem_k.at[4], sem_k.at[5], sibling)
+    local_wait(v4.at[pl.ds(0, 3), pl.ds(0, 64)], sem_k.at[3])
+    values_in = v4.at[:, pl.ds(pl.multiple_of(c * 64, 64), 64)]
+    remote(values_in, values_in, sem_k.at[7], sem_k.at[6], sibling)
+
+    @pl.when(x != y)
+    def _():
+        local_wait(tgt_half, sem_t.at[3])
+        remote(tgt_half, tgt_half, sem_t.at[6], sem_t.at[7], sibling)
+
     row = lax.broadcasted_iota(jnp.int32, (tokens_n, tokens_n), 0)
     col = lax.broadcasted_iota(jnp.int32, (tokens_n, tokens_n), 1)
+
+    to_log2 = HEAD_DIM ** (-0.5) * math.log2(math.e)
 
     def attend(xb):
         @pl.loop(0, NY)
@@ -355,16 +380,16 @@
             query = base + noise_scale * shift
             for j in range(2):
                 q = turned(query[j * HEAD_DIM : (j + 1) * HEAD_DIM]).astype(bf16)
-                scores = jnp.dot(k4[yh], q, preferred_element_type=f32) * HEAD_DIM ** (-0.5)
+                scores = jnp.dot(k4[yh], q, preferred_element_type=f32)
                 scores = jnp.where(row <= col, scores, -1e30)
-                scores = jnp.exp(scores - jnp.max(scores, axis=0, keepdims=True))
-                probs = scores / jnp.sum(scores, axis=0, keepdims=True)
-                mixed = jnp.dot(v4[yh], probs.astype(bf16), preferred_element_type=f32)
+                scores = jnp.exp2((scores - jnp.max(scores, axis=0, keepdims=True)) * to_log2)
+                share = 1.0 / jnp.sum(scores, axis=0, keepdims=True)
+                mixed = jnp.dot(v4[yh], (scores * share).astype(bf16), preferred_element_type=f32)
                 mt[yh, xb * 2 + j] = mixed.astype(bf16)
 
     local_wait(bt.at[:, x, :, 1 - c], sem_4.at[1])
-    for k in (1, 3):
-        local_wait(k4.at[pl.ds(0, 3)] if k == 1 else v4.at[pl.ds(0, 3)], sem_k.at[k])
+    local_wait(k4.at[:, pl.ds(0, 128)], sem_k.at[5])
+    local_wait(v4.at[:, pl.ds(0, 64)], sem_k.at[6])
 
     @pl.when(x != y)
     def _():
@@ -401,34 +426,54 @@
     wide.far()
     chip = x * NZ + z
     own = fac_all.at[chip, c]
-    loads["own"].wait()
 
     @pl.loop(1, NX * NZ)
     def _(i):
         to = (chip + i) % (NX * NZ)
-        remote(own, own, sem_f.at[0], sem_f.at[1], (to // NZ, to % NZ, c, y))
+        remote(fac, own, sem_f.at[0], sem_f.at[1], (to // NZ, to % NZ, c, y))
+
+    @pl.loop(1, PLANE)
+    def _(i):
+        to = (p + i) % PLANE
+        remote(left_in.at[to], left_out.at[p], sem_g.at[0], sem_g.at[1], plane_device(to, y))
 
     block_use(1)
     block_use(3)
     block_use(2)
 
+    out_right = lft_m[pl.ds(RANK, RANK), pl.ds(pl.multiple_of(x * COLS, 128), COLS)].astype(f32)
+    beside = jnp.concatenate([out_right] * 3 + [jnp.zeros((128 - 3 * RANK, COLS), f32)], axis=0)
+    beside = beside.T.astype(bf16).reshape(NZ, NC, ROWS, 128)
+    for b in range(NY):
+        wbuf[b, :, :, :, pl.ds(COLS, 128)] = beside
+
+    @pl.when(x != y)
+    def _():
+        local_wait(tgt.at[pl.ds(0, 128)], sem_t.at[7])
+
+    tgt_t[...] = tgt[...].astype(f32).T
+
     wide.finish()
-    out_right = lft_m[pl.ds(RANK, RANK), pl.ds(pl.multiple_of(x * COLS, 128), COLS)].astype(f32)
     acc[...] = -tgt_t[...]
 
     @pl.loop(0, NY)
     def _(b):
         rows = mt[b, pl.ds(0, 7)].reshape(COLS, tokens_n)
-        term = jnp.dot(wbuf[b].reshape(COLS, COLS), rows, preferred_element_type=f32)
-        low_o = jnp.dot(fb[b, pl.ds(RANK, RANK), pl.ds(0, COLS)], rows, preferred_element_type=f32)
-        shift = lax.dot_general(
-            out_right,
-            low_o,
-            (((0,), (0,)), ((), ())),
-            precision=lax.Precision.HIGHEST,
+        low_o = noise_scale * jnp.dot(
+            fb[b, pl.ds(RANK, RANK), pl.ds(0, COLS)], rows, preferred_element_type=f32
+        )
+        first = low_o.astype(bf16).astype(f32)
+        second = (low_o - first).astype(bf16).astype(f32)
+        third = low_o - first - second
+        low_parts = jnp.concatenate(
+            [first, second, third, jnp.zeros((128 - 3 * RANK, tokens_n), f32)], axis=0
+        ).astype(bf16)
+        term = jnp.dot(
+            wbuf[b].reshape(COLS, COLS + 128),
+            jnp.concatenate([rows, low_parts], axis=0),
             preferred_element_type=f32,
         )
-        acc[...] += (term + noise_scale * shift).astype(bf16).astype(f32)
+        acc[...] += term.astype(bf16).astype(f32)
 
     part[x] = jnp.full((1, 128), jnp.sum(acc[...] * acc[...]), f32)
     for d in range(1, NX):
@@ -451,24 +496,57 @@
             (x, (to // NC) % NZ, to % NC, to // (NZ * NC)),
         )
 
+    local_wait(left_out.at[pl.ds(0, PLANE - 1)], sem_g.at[1])
+    local_wait(fac_all.at[:, 1 - c], sem_f.at[3])
     local_wait(ev.at[pl.ds(0, PLANE - 1)], sem_e.at[3])
-    local_wait(fac_all.at[:, 1 - c], sem_f.at[3])
+
+    scored = -(ev[...].reshape(PLANE, 128) / (tokens_n * D))
+    mean = jnp.sum(scored, axis=0, keepdims=True) / PLANE
+    apart = scored - mean
+    spread = jnp.sum(apart * apart, axis=0, keepdims=True) / PLANE
+    weight = apart / jnp.sqrt(spread + spread_floor) / noise_scale
+    fit[...] = -(ev[p] / (tokens_n * D))
+    rank_at = lax.broadcasted_iota(jnp.int32, (PLANE, 8, 128), 1)
+    left = left_out[...].astype(f32) * weight[:, None, :]
+    left = jnp.concatenate(
+        [
+            jnp.where(rank_at < RANK, left, 0.0).reshape(PLANE * 8, 128),
+            jnp.where(rank_at < RANK, 0.0, left).reshape(PLANE * 8, 128),
+        ],
+        axis=1,
+    )
+    right = fac_all[...].reshape(PLANE * 8, COLS)
+    first = left.astype(bf16)
+    rest = left - first.astype(f32)
+    second = rest.astype(bf16)
+    third = (rest - second.astype(f32)).astype(bf16)
+    grads = jnp.zeros((256, COLS), f32)
+    for piece in (third, second, first):
+        grads += lax.dot_general(
+            piece, right, (((0,), (0,)), ((), ())), preferred_element_type=f32
+        )
+    grad_q[...] = grads[:ROWS]
+    grad_o[...] = grads[128 : 128 + ROWS]
 
     wide.drain()
-    local_wait(s_out.at[pl.ds(0, PLANE - 1)], sem_s.at[0])
+    local_wait(slab_out.at[pl.ds(0, PLANE - 1)], sem_s.at[0])
+    local_wait(left_out.at[pl.ds(0, PLANE - 1)], sem_g.at[0])
 
     @pl.when(x != y)
     def _():
         local_wait(lft_m, sem_t.at[0])
-        local_wait(tgt_m, sem_t.at[2])
+        local_wait(tgt.at[pl.ds(0, 128)], sem_t.at[6])
         local_wait(fb.at[:, :, pl.ds(0, COLS)], sem_t.at[4])
 
     @pl.when(x == y)
     def _():
+        local_wait(tok.at[pl.ds(0, 3 * 128 * COLS // D)], sem_t.at[2])
         local_wait(fb.at[pl.ds(0, 3), :, pl.ds(0, COLS)], sem_t.at[4])
 
-    local_wait(k4.at[pl.ds(0, 3)], sem_k.at[0])
-    local_wait(v4.at[pl.ds(0, 3)], sem_k.at[2])
+    local_wait(k4.at[pl.ds(0, 3), pl.ds(0, 128)], sem_k.at[0])
+    local_wait(v4.at[pl.ds(0, 3), pl.ds(0, 64)], sem_k.at[2])
+    local_wait(k4.at[:, pl.ds(0, 128)], sem_k.at[4])
+    local_wait(v4.at[:, pl.ds(0, 64)], sem_k.at[7])
     local_wait(bt.at[pl.ds(0, 3), 0, 0, 0], sem_1.at[0])
     local_wait(bt.at[:, 0, pl.ds(0, 7), 0], sem_2.at[0])
     local_wait(bt.at[:, pl.ds(0, 3), :, 0], sem_3.at[0])
@@ -479,53 +557,62 @@
     local_wait(ev.at[pl.ds(0, PLANE - 1)], sem_e.at[2])
 
 
-def forward(tokens, w_key, w_value, wo_t, target, s_in, fac, lft, cos_t, sin_t):
-    tok = tokens.shape[0]
+def forward(ids, *ins):
+    tok = ins[0].shape[0]
     bf16, f32 = jnp.bfloat16, jnp.float32
-    ins = (tokens, w_key, w_value, wo_t, target, s_in, fac, lft, cos_t, sin_t)
-    held = (tokens, w_key, w_value, target, s_in, fac, lft, cos_t, sin_t)
+    held = [a for i, a in enumerate(ins) if i not in (3,)]
+    order = (0, 1, 2, 3, 4, 5, 6, 7, 8, 9, 10)
     dma = pltpu.SemaphoreType.DMA
     return pl.pallas_call(
         forward_kernel,
         name="forward",
         out_shape=(
-            jax.ShapeDtypeStruct((PLANE, 1, 128), f32),
-            jax.ShapeDtypeStruct((NX * NZ, NC, 8, COLS), bf16),
-            jax.ShapeDtypeStruct(s_in.shape, bf16),
+            jax.ShapeDtypeStruct((ROWS, COLS), f32),
+            jax.ShapeDtypeStruct((ROWS, COLS), f32),
+            jax.ShapeDtypeStruct((1, 128), f32),
         ),
-        in_specs=[pl.BlockSpec(memory_space=pl.ANY)] * len(ins),
+        in_specs=[pl.BlockSpec(memory_space=pltpu.SMEM)]
+        + [pl.BlockSpec(memory_space=pl.ANY)] * len(ins),
         out_specs=[pl.BlockSpec(memory_space=pltpu.VMEM)] * 3,
-        scratch_shapes=[pltpu.VMEM(a.shape, a.dtype) for a in held]
+        scratch_shapes=[pltpu.VMEM(held[i].shape, held[i].dtype) for i in order]
         + [
-            pltpu.VMEM((NY, NZ, NC, ROWS, COLS), bf16),
+            pltpu.VMEM((PLANE, SLAB, 128), bf16),
+            pltpu.VMEM((PLANE, SLAB, 128), bf16),
+            pltpu.VMEM((PLANE, 8, 128), bf16),
+            pltpu.VMEM((PLANE, 8, 128), bf16),
+            pltpu.VMEM((8, COLS), bf16),
+            pltpu.VMEM((NX * NZ, NC, 8, COLS), bf16),
+            pltpu.VMEM((8, D), bf16),
+            pltpu.VMEM((PLANE, 1, 128), f32),
+            pltpu.VMEM((NY, NZ, NC, ROWS, COLS + 128), bf16),
             pltpu.VMEM((NY, NX, NZ, NC, SLAB, tok), bf16),
             pltpu.VMEM((NY, 8, HEAD_DIM, tok), bf16),
             pltpu.VMEM((NY, tok, HEAD_DIM), bf16),
             pltpu.VMEM((NY, HEAD_DIM, tok), bf16),
             pltpu.VMEM((NY, 8, COLS + 128), bf16),
             pltpu.VMEM((8, D), bf16),
-            pltpu.VMEM((tok, COLS), bf16),
             pltpu.VMEM((COLS, tok), f32),
             pltpu.VMEM((COLS, tok), f32),
             pltpu.VMEM((8, tok), bf16),
             pltpu.VMEM((NX, 1, 128), f32),
             pltpu.VMEM((1, 128), f32),
-            dma((11,)),
+            dma((12,)),
             dma((PlaneGather.SEMS,)),
             dma((2,)),
-            dma((6,)),
-            dma((4,)),
+            dma((8,)),
+            dma((8,)),
             dma((2,)),
             dma((8,)),
             dma((4,)),
             dma((5,)),
             dma((4,)),
             dma((4,)),
+            dma((2,)),
         ],
         compiler_params=pltpu.CompilerParams(
             collective_id=0, has_side_effects=True, vmem_limit_bytes=60 * 1024 * 1024
         ),
-    )(*ins)
+    )(ids, *ins)
 
 
 def tables(count, head_size):
@@ -549,43 +636,23 @@
     o_right,
     member_ids,
 ):
-    tok = tokens.shape[0]
-    f32, bf16 = jnp.float32, jnp.bfloat16
-    cos_t, sin_t = tables(tok, HEAD_DIM)
-    signs = (1 - 2 * (member_ids % 2)).astype(bf16)
-    lft = jnp.concatenate([jnp.transpose(query_left_factors[0]), o_right[0]], axis=0) * signs
-    fac = jnp.concatenate([query_right_factors[0], jnp.transpose(o_left[0])], axis=0)
-    slabs = jnp.transpose(w_query).reshape(COLS // SLAB, SLAB, ROWS)
-    slabs = jnp.pad(slabs, ((0, PLANE - COLS // SLAB), (0, 0), (0, 128 - ROWS)))
-    lefts = jnp.transpose(lft.reshape(2 * RANK, PLANE, ROWS), (1, 0, 2))
-    lefts = jnp.pad(lefts, ((0, 0), (0, 0), (0, 128 - ROWS)))
-    s_in = jnp.concatenate([slabs, lefts], axis=1)
-    errors, facs, s_out = forward(
-        tokens, w_key, w_value, jnp.transpose(w_out), target, s_in, fac, lft, cos_t, sin_t
+    cos_t, sin_t = tables(tokens.shape[0], HEAD_DIM)
+    grad_q, grad_o, fit = forward(
+        member_ids,
+        tokens,
+        w_key,
+        w_value,
+        jnp.transpose(w_out),
+        target,
+        w_query,
+        jnp.transpose(query_left_factors[0]),
+        query_right_factors[0],
+        jnp.transpose(o_left[0]),
+        o_right[0],
+        cos_t,
+        sin_t,
     )
-    everyone = -(errors[:, 0, 0] / (tok * D))
-    p = (lax.axis_index(POP[0]) * NZ + lax.axis_index(POP[1])) * NC + lax.axis_index(POP[2])
-    fitness = lax.dynamic_slice(everyone, (p,), (1,))
-    mean = jnp.sum(everyone) / PLANE
-    spread = jnp.sum((everyone - mean) * (everyone - mean)) / PLANE
-    unsigned = (everyone - mean) / jnp.sqrt(spread + spread_floor)
-    lefts = s_out[:, SLAB:, :ROWS].astype(f32) * unsigned[:, None, None]
-    rights = facs.reshape(PLANE, 2 * RANK, COLS).astype(f32)
-
-    def gradient(left, right):
-        return (
-            lax.dot_general(
-                left.reshape(-1, ROWS),
-                right.reshape(-1, COLS),
-                (((0,), (0,)), ((), ())),
-                precision=lax.Precision.HIGHEST,
-            )
-            / noise_scale
-        )
-
-    grad_query = gradient(lefts[:, :RANK], rights[:, :RANK])
-    grad_out = gradient(lefts[:, RANK:], rights[:, RANK:])
-    return (grad_query, jnp.transpose(grad_out), fitness)
+    return (grad_q, jnp.transpose(grad_o), fit[0, :1])
 
 
 def solution(mesh):

time: 122 us -> 92.3 us (0.76)
  Pallas kernels: 105 us -> 85.9 us
  other arithmetic: 6.67 us -> 0 us
  matrix products: 2.12 us -> 0 us
  local copies, waits for them, and re-layouts: 5.33 us -> 3.24 us
    pallas_call x1, Pallas kernels: 105 us -> 85.9 us  [forward(): pl.pallas_call(forward_kernel, name='forward', out_shape=(jax.ShapeDtypeS...]
    unnamed x8 -> x2, local copies, waits for them, and re-layouts: 0.02 us -> 3.24 us
    reduce_sum x2 -> x0, other arithmetic: 2.87 us -> none  [the longest x1 1.43 us: per_device(): spread = jnp.sum((everyone - mean) * (everyone - mean)) / PLANE]
    dot_general x2 -> x0, matrix products: 2.12 us -> none  [gradient(): lax.dot_general(left.reshape(-1, ROWS), right.reshape(-1, COLS), (((0,),...]
    concatenate x4 -> x0, local copies, waits for them, and re-layouts: 1.89 us -> none  [per_device(): jnp.concatenate([jnp.transpose(query_left_factors[0]), o_right[0]], axis=0)]
    slice x2 -> x0, local copies, waits for them, and re-layouts: 1.86 us -> none  [per_device(): grad_out = gradient(lefts[:, RANK:], rights[:, RANK:])]
    mul x2 -> x0, other arithmetic: 1.69 us -> none  [the longest x1 1.03 us: per_device(): lefts = s_out[:, SLAB:, :ROWS].astype(f32) * unsigned[:, None, None]]
    concatenate x2 -> x0, other arithmetic: 1.45 us -> none  [the longest x1 0.84 us: per_device(): s_in = jnp.concatenate([slabs, lefts], axis=1)]
where the time goes in v3:
time: 92.3 us; the launch traced here: 92.1 us
  Pallas kernels  85.9 us (93%)
  local copies, waits for them, and re-layouts  3.24 us (4%)
  between operations  2.99 us (3%)
    pallas_call x1, Pallas kernels, forward(): pl.pallas_call(forward_kernel, name='forward', out_shape=(jax.ShapeDtypeS...  85.9 us
    unnamed x2, local copies, waits for them, and re-layouts  3.24 us

profile of v3, /device:TPU:1, one launch (start us, length us, event | category | flops | bytes accessed | tf_op | source)
XLA Modules:
  0.0 92.1 jit_solution(11899699967218712164)
XLA Ops:
  1.3 85.9 %forward.1 = (f32[56,896]{1,0:T(8,128)}, f32[56,896]{1,0:T(8,128)}, f32[1,128]{1,0:T(1,128)}) custom-call(s32[1]{0:T(128)S(6)} %copy.19.ids, bf16[256,3584]{1,0:T(8,128)(2,1)} %tok_h.1, bf16[3584,128]{1,0:T(8,128)(2,1)} %wk_h.1, bf16[3584,128]{1,0:T(8,128)(2,1)} %wv_h.1, bf16[56,896]{1,0:T(8,128)(2,1)} %bitcast.13, bf16[256,896]{1,0:T(8,128)(2,1)} %tgt_h.1, ...), custom_call_target="tpu_custom_call" | custom-call | tf_op jit(solution)/shard_map/forward/pallas_call | solution.py:566
  87.2 1.6 %copy.20 = f32[56,896]{1,0:T(8,128)} copy(f32[56,896]{1,0:T(8,128)} %get-tuple-element.12) | data formatting | bytes 401408
  88.8 1.6 %copy.21 = f32[896,56]{0,1:T(8,128)} copy(f32[896,56]{0,1:T(8,128)} %bitcast.12) | data formatting | bytes 401408

commit v4 on v3

--- a/solution.py
+++ b/solution.py
@@ -31,8 +31,8 @@
     return tuple(lax.axis_index(a) for a in AXES)
 
 
-def plane_device(p, y):
-    return (p // (NZ * NC), (p // NC) % NZ, p % NC, y)
+PEERS = [(d, dz, dc) for d in (2, 1, 3, 0) for dz in (4, 3, 5, 2, 6, 1, 7, 0) for dc in (1, 0)]
+PEERS.remove((0, 0, 0))
 
 
 def local_wait(ref, sem):
@@ -161,9 +161,8 @@
         local_wait(self.buf.at[:, :, self.c, :, pl.ds(0, COLS)], self.sem.at[4])
 
 
-CUT = 256
+CUT = 512
 SLAB = 16
-FAR_FIRST = (1, 7, 2, 6, 3, 5, 4)
 
 
 def remote(src, dst, ssem, rsem, to):
@@ -213,13 +212,12 @@
     def greet(to):
         pl.semaphore_signal(barrier, inc=1, device_id=to, device_id_type=MESH)
 
-    @pl.loop(1, PLANE)
-    def _(i):
-        greet(plane_device((p + i) % PLANE, y))
-
-    @pl.loop(0, 3 * NZ * NC)
-    def _(i):
-        greet((x, (i // NC) % NZ, i % NC, (y + 1 + i // (NZ * NC)) % NY))
+    for dx, dz, dc in PEERS:
+        greet(((x + dx) % NX, (z + dz) % NZ, (c + dc) % NC, y))
+
+    for dy, dz, dc in PEERS:
+        if dy:
+            greet((x, (z + dz) % NZ, (c + dc) % NC, (y + dy) % NY))
 
     for dx in range(1, NX):
         for dy in range(1, NY):
@@ -233,11 +231,11 @@
     sign = (1 - 2 * (ids[0] % 2)).astype(f32)
     for name in ("wq", "ql", "or", "qr", "ol"):
         loads[name].wait()
-    slab_in[pl.ds(0, COLS // SLAB), :, pl.ds(0, ROWS)] = (
-        wq[...].astype(f32).T.reshape(COLS // SLAB, SLAB, ROWS).astype(bf16)
-    )
+    slabs = wq[...].astype(f32).T.reshape(COLS // SLAB, 2, 8, ROWS).astype(bf16)
+    for i in range(2):
+        slab_in[pl.ds(0, COLS // SLAB), :, pl.ds(i * ROWS, ROWS)] = slabs[:, i]
     slab_in[pl.ds(COLS // SLAB, PLANE - COLS // SLAB)] = jnp.zeros(
-        (PLANE - COLS // SLAB, SLAB, 128), bf16
+        (PLANE - COLS // SLAB, 8, 128), bf16
     )
     fac[...] = jnp.concatenate([qr[...].astype(f32), ol[...].astype(f32)], axis=0).astype(bf16)
     lft[...] = (jnp.concatenate([ql[...].astype(f32), orr[...].astype(f32)], axis=0) * sign).astype(bf16)
@@ -257,10 +255,12 @@
     loads["tgt"].wait()
     pl.semaphore_wait(barrier, PLANE - 1 + 3 * NZ * NC + 9)
 
-    @pl.loop(1, PLANE)
-    def _(i):
-        to = (p + i) % PLANE
-        remote(slab_in.at[to], slab_out.at[p], sem_s.at[0], sem_s.at[1], plane_device(to, y))
+    def to_plane(src, dst, sem):
+        for dx, dz, dc in PEERS:
+            xx, zz, cc = (x + dx) % NX, (z + dz) % NZ, (c + dc) % NC
+            remote(src.at[(xx * NZ + zz) * NC + cc], dst.at[p], sem.at[0], sem.at[1], (xx, zz, cc, y))
+
+    to_plane(slab_in, slab_out, sem_s)
 
     @pl.when(x != y)
     def _():
@@ -280,31 +280,54 @@
     def _():
         lft_m[...] = lft[...]
 
-    wide.a_line()
-
     @pl.when(x != y)
     def _():
         local_wait(lft_m, sem_t.at[1])
 
     local_wait(slab_out.at[pl.ds(0, PLANE - 1)], sem_s.at[1])
-    slab = jnp.concatenate([slab_out[i, :, pl.ds(0, ROWS)] for i in range(PLANE)], axis=1)
     made = lax.dot_general(
-        jnp.concatenate([slab, lft_m[...]], axis=0),
+        jnp.concatenate(
+            [
+                jnp.concatenate(
+                    [slab_out[i, :, pl.ds(h * ROWS, ROWS)] for i in range(PLANE)], axis=1
+                )
+                for h in range(2)
+            ]
+            + [lft_m[...]],
+            axis=0,
+        ),
         tok[...],
         (((1,), (1,)), ((), ())),
         preferred_element_type=f32,
     )
     bt[y, x, z, c] = made[:SLAB].astype(bf16)
     low[...] = made[SLAB : SLAB + 8].astype(bf16)
-    for d in range(1, NY):
-        own = bt.at[y, x, z, c]
-        remote(own, own, sem_1.at[0], sem_1.at[1], (x, z, c, (y + d) % NY))
+    mine = bt.at[y, x, z, c]
+    for d in (4, 3, 5, 2, 6, 1, 7):
+        remote(mine, mine, sem_1.at[0], sem_1.at[1], (x, (z + d) % NZ, c, y))
+
+    wide.a_line()
+    wide.b_step(1)
+    wide.y_step(0)
+
+    local_wait(bt.at[y, x, pl.ds(0, 7), c], sem_1.at[1])
+
+    def line_out(yy):
+        ref = bt.at[yy, x, :, c]
+        for d in (1, 3, 2):
+            remote(ref, ref, sem_3.at[0], sem_3.at[d], ((x + d) % NX, z, c, y))
+        remote(ref, ref, sem_4.at[0], sem_4.at[1], sibling)
+
+    line = bt.at[y, x, :, c]
+    for d in (2, 1, 3):
+        remote(line, line, sem_2.at[0], sem_2.at[d], (x, z, c, (y + d) % NY))
+    line_out(y)
 
     tgt_half = tgt.at[pl.ds(pl.multiple_of(c * 128, 128), 128)]
 
     @pl.when(x == y)
     def _():
-        for d in range(1, NY):
+        for d in (2, 1, 3):
             to = (x, z, c, (y + d) % NY)
             remote(tgt_half, tgt_half, sem_t.at[2], sem_t.at[3], to)
 
@@ -321,36 +344,20 @@
     def _():
         fb[y, :, pl.ds(0, COLS)] = fac[...]
 
-    wide.b_step(1)
-    wide.y_step(0)
-
-    local_wait(bt.at[pl.ds(0, 3), 0, 0, 0], sem_1.at[1])
-
-    def line_out(zz):
-        ref = bt.at[:, x, zz, c]
-        for d in (1, 3, 2):
-            remote(ref, ref, sem_3.at[0], sem_3.at[d], ((x + d) % NX, z, c, y))
-        remote(ref, ref, sem_4.at[0], sem_4.at[1], (x, z, 1 - c, y))
-
-    mine = bt.at[:, x, z, c]
-    for d in FAR_FIRST:
-        remote(mine, mine, sem_2.at[0], sem_2.at[d], (x, (z + d) % NZ, c, y))
-    line_out(z)
-
-    def line_in(d):
-        zz = (z + NZ - d) % NZ
-        local_wait(bt.at[:, x, zz, c], sem_2.at[d])
-        line_out(zz)
-
     wide.a_step(1)
-    for d in FAR_FIRST[:3]:
-        line_in(d)
     wide.b_step(2)
     wide.y_step(1)
     wide.y_step(2)
-    for d in FAR_FIRST[3:]:
-        line_in(d)
+
+    for d in (1, 3, 2):
+        yy = (y + NY - d) % NY
+        local_wait(bt.at[yy, x, :, c], sem_2.at[d])
+        line_out(yy)
+
+    wide.b_step(3)
     wide.a_step(2)
+    wide.y_step(3)
+    wide.y_step(4)
 
     local_wait(k4.at[pl.ds(0, 3), pl.ds(0, 128)], sem_k.at[1])
     keys_in = k4.at[:, pl.ds(pl.multiple_of(c * 128, 128), 128)]
@@ -358,34 +365,29 @@
     local_wait(v4.at[pl.ds(0, 3), pl.ds(0, 64)], sem_k.at[3])
     values_in = v4.at[:, pl.ds(pl.multiple_of(c * 64, 64), 64)]
     remote(values_in, values_in, sem_k.at[7], sem_k.at[6], sibling)
-
-    @pl.when(x != y)
-    def _():
-        local_wait(tgt_half, sem_t.at[3])
-        remote(tgt_half, tgt_half, sem_t.at[6], sem_t.at[7], sibling)
-
     row = lax.broadcasted_iota(jnp.int32, (tokens_n, tokens_n), 0)
     col = lax.broadcasted_iota(jnp.int32, (tokens_n, tokens_n), 1)
 
     to_log2 = HEAD_DIM ** (-0.5) * math.log2(math.e)
 
     def attend(xb):
-        @pl.loop(0, NY)
-        def _(yh):
-            right = fb[yh, pl.ds(0, RANK), pl.ds(pl.multiple_of(xb * 256, 256), 256)]
-            shift = lax.dot_general(
-                right, low[pl.ds(0, RANK), :], (((0,), (0,)), ((), ())), preferred_element_type=f32
-            )
-            base = bt[yh, xb].reshape(2 * HEAD_DIM, tokens_n).astype(f32)
-            query = base + noise_scale * shift
-            for j in range(2):
-                q = turned(query[j * HEAD_DIM : (j + 1) * HEAD_DIM]).astype(bf16)
-                scores = jnp.dot(k4[yh], q, preferred_element_type=f32)
-                scores = jnp.where(row <= col, scores, -1e30)
-                scores = jnp.exp2((scores - jnp.max(scores, axis=0, keepdims=True)) * to_log2)
-                share = 1.0 / jnp.sum(scores, axis=0, keepdims=True)
-                mixed = jnp.dot(v4[yh], (scores * share).astype(bf16), preferred_element_type=f32)
-                mt[yh, xb * 2 + j] = mixed.astype(bf16)
+        @pl.loop(0, NY, step=2)
+        def _(pair):
+            for yh in (pair, pair + 1):
+                right = fb[yh, pl.ds(0, RANK), pl.ds(pl.multiple_of(xb * 256, 256), 256)]
+                shift = lax.dot_general(
+                    right, low[pl.ds(0, RANK), :], (((0,), (0,)), ((), ())), preferred_element_type=f32
+                )
+                base = bt[yh, xb].reshape(2 * HEAD_DIM, tokens_n).astype(f32)
+                query = base + noise_scale * shift
+                for j in range(2):
+                    q = turned(query[j * HEAD_DIM : (j + 1) * HEAD_DIM]).astype(bf16)
+                    scores = jnp.dot(k4[yh], q, preferred_element_type=f32)
+                    scores = jnp.where(row <= col, scores, -1e30)
+                    scores = jnp.exp2((scores - jnp.max(scores, axis=0, keepdims=True)) * to_log2)
+                    share = 1.0 / jnp.sum(scores, axis=0, keepdims=True)
+                    mixed = jnp.dot(v4[yh], (scores * share).astype(bf16), preferred_element_type=f32)
+                    mt[yh, xb * 2 + j] = mixed.astype(bf16)
 
     local_wait(bt.at[:, x, :, 1 - c], sem_4.at[1])
     local_wait(k4.at[:, pl.ds(0, 128)], sem_k.at[5])
@@ -400,15 +402,15 @@
         local_wait(fb.at[pl.ds(0, 3), :, pl.ds(0, COLS)], sem_t.at[5])
 
     attend(x)
-    wide.b_step(3)
-    wide.y_step(3)
-    wide.y_step(4)
     wide.a_step(3)
+    wide.b_step(4)
+    wide.y_step(5)
+    wide.y_step(6)
 
     def block_in(d):
         ref = bt.at[:, (x + NX - d) % NX, :, c]
         local_wait(ref, sem_3.at[d])
-        remote(ref, ref, sem_4.at[0], sem_4.at[1 + d], (x, z, 1 - c, y))
+        remote(ref, ref, sem_4.at[0], sem_4.at[1 + d], sibling)
 
     def block_use(d):
         xb = (x + NX - d) % NX
@@ -417,29 +419,28 @@
 
     block_in(1)
     block_in(3)
-    wide.b_step(4)
-    wide.y_step(5)
-    wide.y_step(6)
+
+    block_use(1)
     wide.a_step(4)
+    chip = x * NZ + z
+    for d in range(1, NZ):
+        remote(fac, fac_all.at[chip, c], sem_f.at[0], sem_f.at[1], (x, (z + d) % NZ, c, y))
+
+    to_plane(left_in, left_out, sem_g)
+    wide.y_step(7)
     block_in(2)
-    wide.y_step(7)
+    block_use(3)
     wide.far()
-    chip = x * NZ + z
-    own = fac_all.at[chip, c]
-
-    @pl.loop(1, NX * NZ)
-    def _(i):
-        to = (chip + i) % (NX * NZ)
-        remote(fac, own, sem_f.at[0], sem_f.at[1], (to // NZ, to % NZ, c, y))
-
-    @pl.loop(1, PLANE)
-    def _(i):
-        to = (p + i) % PLANE
-        remote(left_in.at[to], left_out.at[p], sem_g.at[0], sem_g.at[1], plane_device(to, y))
-
-    block_use(1)
-    block_use(3)
+    @pl.when(x != y)
+    def _():
+        local_wait(tgt_half, sem_t.at[3])
+        remote(tgt_half, tgt_half, sem_t.at[6], sem_t.at[7], sibling)
+
     block_use(2)
+    local_wait(fac_all.at[pl.ds(0, NZ - 1), c], sem_f.at[1])
+    facs = fac_all.at[pl.ds(x * NZ, NZ), c]
+    for d in range(1, NX):
+        remote(facs, facs, sem_f.at[2], sem_f.at[3], ((x + d) % NX, z, c, y))
 
     out_right = lft_m[pl.ds(RANK, RANK), pl.ds(pl.multiple_of(x * COLS, 128), COLS)].astype(f32)
     beside = jnp.concatenate([out_right] * 3 + [jnp.zeros((128 - 3 * RANK, COLS), f32)], axis=0)
@@ -478,26 +479,19 @@
     part[x] = jnp.full((1, 128), jnp.sum(acc[...] * acc[...]), f32)
     for d in range(1, NX):
         remote(part.at[x], part.at[x], sem_e.at[0], sem_e.at[1], ((x + d) % NX, z, c, y))
-    local_wait(fac_all.at[pl.ds(0, NX * NZ - 1), c], sem_f.at[1])
-    remote(fac_all.at[:, c], fac_all.at[:, c], sem_f.at[2], sem_f.at[3], (x, z, 1 - c, y))
+    local_wait(fac_all.at[pl.ds(0, 3 * NZ), c], sem_f.at[3])
+    remote(fac_all.at[:, c], fac_all.at[:, c], sem_f.at[4], sem_f.at[5], sibling)
     local_wait(part.at[pl.ds(0, NX - 1)], sem_e.at[1])
     total[...] = part[0] + part[1] + part[2] + part[3]
     slot = (y * NZ + z) * NC + c
     ev[slot] = total[...]
 
-    @pl.loop(1, PLANE)
-    def _(i):
-        to = (slot + i) % PLANE
-        remote(
-            total,
-            ev.at[slot],
-            sem_e.at[2],
-            sem_e.at[3],
-            (x, (to // NC) % NZ, to % NC, to // (NZ * NC)),
-        )
+    for dy, dz, dc in PEERS:
+        to = (x, (z + dz) % NZ, (c + dc) % NC, (y + dy) % NY)
+        remote(total, ev.at[slot], sem_e.at[2], sem_e.at[3], to)
 
     local_wait(left_out.at[pl.ds(0, PLANE - 1)], sem_g.at[1])
-    local_wait(fac_all.at[:, 1 - c], sem_f.at[3])
+    local_wait(fac_all.at[:, 1 - c], sem_f.at[5])
     local_wait(ev.at[pl.ds(0, PLANE - 1)], sem_e.at[3])
 
     scored = -(ev[...].reshape(PLANE, 128) / (tokens_n * D))
@@ -547,12 +541,13 @@
     local_wait(v4.at[pl.ds(0, 3), pl.ds(0, 64)], sem_k.at[2])
     local_wait(k4.at[:, pl.ds(0, 128)], sem_k.at[4])
     local_wait(v4.at[:, pl.ds(0, 64)], sem_k.at[7])
-    local_wait(bt.at[pl.ds(0, 3), 0, 0, 0], sem_1.at[0])
-    local_wait(bt.at[:, 0, pl.ds(0, 7), 0], sem_2.at[0])
+    local_wait(bt.at[0, 0, pl.ds(0, 7), 0], sem_1.at[0])
+    local_wait(bt.at[pl.ds(0, 3), 0, :, 0], sem_2.at[0])
     local_wait(bt.at[:, pl.ds(0, 3), :, 0], sem_3.at[0])
     local_wait(bt.at[:, :, :, 0], sem_4.at[0])
-    local_wait(fac_all.at[pl.ds(0, NX * NZ - 1), c], sem_f.at[0])
-    local_wait(fac_all.at[:, c], sem_f.at[2])
+    local_wait(fac_all.at[pl.ds(0, NZ - 1), c], sem_f.at[0])
+    local_wait(fac_all.at[pl.ds(0, 3 * NZ), c], sem_f.at[2])
+    local_wait(fac_all.at[:, c], sem_f.at[4])
     local_wait(part.at[pl.ds(0, NX - 1)], sem_e.at[0])
     local_wait(ev.at[pl.ds(0, PLANE - 1)], sem_e.at[2])
 
@@ -576,8 +571,8 @@
         out_specs=[pl.BlockSpec(memory_space=pltpu.VMEM)] * 3,
         scratch_shapes=[pltpu.VMEM(held[i].shape, held[i].dtype) for i in order]
         + [
-            pltpu.VMEM((PLANE, SLAB, 128), bf16),
-            pltpu.VMEM((PLANE, SLAB, 128), bf16),
+            pltpu.VMEM((PLANE, 8, 128), bf16),
+            pltpu.VMEM((PLANE, 8, 128), bf16),
             pltpu.VMEM((PLANE, 8, 128), bf16),
             pltpu.VMEM((PLANE, 8, 128), bf16),
             pltpu.VMEM((8, COLS), bf16),
@@ -602,10 +597,10 @@
             dma((8,)),
             dma((8,)),
             dma((2,)),
-            dma((8,)),
+            dma((4,)),
             dma((4,)),
             dma((5,)),
-            dma((4,)),
+            dma((6,)),
             dma((4,)),
             dma((2,)),
         ],

time: 92.3 us -> 79.4 us (0.86)
  Pallas kernels: 85.9 us -> 73 us
    pallas_call x1, Pallas kernels: 85.9 us -> 73 us  [forward(): pl.pallas_call(forward_kernel, name='forward', out_shape=(jax.ShapeDtypeS...]
where the time goes in v4:
time: 79.4 us; the launch traced here: 79.3 us
  Pallas kernels  73 us (92%)
  local copies, waits for them, and re-layouts  3.24 us (4%)
  between operations  2.99 us (4%)
    pallas_call x1, Pallas kernels, forward(): pl.pallas_call(forward_kernel, name='forward', out_shape=(jax.ShapeDtypeS...  73 us
    unnamed x2, local copies, waits for them, and re-layouts  3.24 us

profile of v4, /device:TPU:1, one launch (start us, length us, event | category | flops | bytes accessed | tf_op | source)
XLA Modules:
  0.0 79.3 jit_solution(5114842914447412244)
XLA Ops:
  1.3 73.0 %forward.1 = (f32[56,896]{1,0:T(8,128)}, f32[56,896]{1,0:T(8,128)}, f32[1,128]{1,0:T(1,128)}) custom-call(s32[1]{0:T(128)S(6)} %copy.19.ids, bf16[256,3584]{1,0:T(8,128)(2,1)} %tok_h.1, bf16[3584,128]{1,0:T(8,128)(2,1)} %wk_h.1, bf16[3584,128]{1,0:T(8,128)(2,1)} %wv_h.1, bf16[56,896]{1,0:T(8,128)(2,1)} %bitcast.13, bf16[256,896]{1,0:T(8,128)(2,1)} %tgt_h.1, ...), custom_call_target="tpu_custom_call" | custom-call | tf_op jit(solution)/shard_map/forward/pallas_call | solution.py:561
  74.3 1.6 %copy.20 = f32[56,896]{1,0:T(8,128)} copy(f32[56,896]{1,0:T(8,128)} %get-tuple-element.12) | data formatting | bytes 401408
  76.0 1.6 %copy.21 = f32[896,56]{0,1:T(8,128)} copy(f32[896,56]{0,1:T(8,128)} %bitcast.12) | data formatting | bytes 401408

commit v5 on v4

--- a/solution.py
+++ b/solution.py
@@ -172,11 +172,11 @@
 
 
 def forward_kernel(
-    ids, tok_h, wk_h, wv_h, wo_h, tgt_h, wq_h, ql_h, qr_h, ol_h, or_h, cos_h, sin_h,
+    ids_h, tok_h, wk_h, wv_h, wo_h, tgt_h, wq_h, ql_h, qr_h, ol_h, or_h, cos_h, sin_h,
     grad_q, grad_o, fit,
     tok, wk, wv, tgt, wq, ql, qr, ol, orr, cos, sin,
     slab_in, slab_out, left_in, left_out, fac, fac_all, lft, ev,
-    wbuf, bt, mt, k4, v4, fb, lft_m, tgt_t, acc, low, part, total,
+    ids, wbuf, bt, mt, k4, v4, fb, lft_m, tgt_t, acc, low, part, total,
     sem_l, sem_w, sem_s, sem_t, sem_k, sem_1, sem_2, sem_3, sem_4, sem_f, sem_e, sem_g,
 ):
     me = place()
@@ -202,6 +202,7 @@
             ("cos", cos_h, cos),
             ("sin", sin_h, sin),
             ("tgt", tgt_h, tgt),
+            ("ids", ids_h, ids),
         )
     ):
         loads[name] = pltpu.make_async_copy(src, dst, sem_l.at[i])
@@ -228,9 +229,9 @@
         ct, st = cos[...], sin[...]
         return jnp.concatenate([first * ct - second * st, second * ct + first * st], axis=0)
 
-    sign = (1 - 2 * (ids[0] % 2)).astype(f32)
-    for name in ("wq", "ql", "or", "qr", "ol"):
+    for name in ("ids", "wq", "ql", "or", "qr", "ol"):
         loads[name].wait()
+    sign = (1 - 2 * (ids[...].reshape(1, 1) % 2)).astype(f32)
     slabs = wq[...].astype(f32).T.reshape(COLS // SLAB, 2, 8, ROWS).astype(bf16)
     for i in range(2):
         slab_in[pl.ds(0, COLS // SLAB), :, pl.ds(i * ROWS, ROWS)] = slabs[:, i]
@@ -344,27 +345,22 @@
     def _():
         fb[y, :, pl.ds(0, COLS)] = fac[...]
 
-    wide.a_step(1)
-    wide.b_step(2)
-    wide.y_step(1)
-    wide.y_step(2)
-
-    for d in (1, 3, 2):
-        yy = (y + NY - d) % NY
-        local_wait(bt.at[yy, x, :, c], sem_2.at[d])
-        line_out(yy)
-
-    wide.b_step(3)
-    wide.a_step(2)
-    wide.y_step(3)
-    wide.y_step(4)
-
     local_wait(k4.at[pl.ds(0, 3), pl.ds(0, 128)], sem_k.at[1])
     keys_in = k4.at[:, pl.ds(pl.multiple_of(c * 128, 128), 128)]
     remote(keys_in, keys_in, sem_k.at[4], sem_k.at[5], sibling)
     local_wait(v4.at[pl.ds(0, 3), pl.ds(0, 64)], sem_k.at[3])
     values_in = v4.at[:, pl.ds(pl.multiple_of(c * 64, 64), 64)]
     remote(values_in, values_in, sem_k.at[7], sem_k.at[6], sibling)
+    for d in (1, 3, 2):
+        yy = (y + NY - d) % NY
+        local_wait(bt.at[yy, x, :, c], sem_2.at[d])
+        line_out(yy)
+
+    wide.a_step(1)
+    wide.b_step(2)
+    wide.y_step(1)
+    wide.y_step(2)
+
     row = lax.broadcasted_iota(jnp.int32, (tokens_n, tokens_n), 0)
     col = lax.broadcasted_iota(jnp.int32, (tokens_n, tokens_n), 1)
 
@@ -402,41 +398,48 @@
         local_wait(fb.at[pl.ds(0, 3), :, pl.ds(0, COLS)], sem_t.at[5])
 
     attend(x)
+    wide.b_step(3)
+    wide.a_step(2)
+    wide.y_step(3)
+    wide.y_step(4)
+
+    chip = x * NZ + z
+    for d in range(1, NZ):
+        remote(fac, fac_all.at[chip, c], sem_f.at[0], sem_f.at[1], (x, (z + d) % NZ, c, y))
+
+
+    def block_in(d):
+        ref = bt.at[:, (x + NX - d) % NX, :, c]
+        local_wait(ref, sem_3.at[d])
+        remote(ref, ref, sem_4.at[0], sem_4.at[1 + d], sibling)
+
+    def block_use(d):
+        xb = (x + NX - d) % NX
+        local_wait(bt.at[:, xb, :, 1 - c], sem_4.at[1 + d])
+        attend(xb)
+
+    block_in(1)
+    block_in(3)
+
+    block_use(1)
     wide.a_step(3)
     wide.b_step(4)
     wide.y_step(5)
     wide.y_step(6)
-
-    def block_in(d):
-        ref = bt.at[:, (x + NX - d) % NX, :, c]
-        local_wait(ref, sem_3.at[d])
-        remote(ref, ref, sem_4.at[0], sem_4.at[1 + d], sibling)
-
-    def block_use(d):
-        xb = (x + NX - d) % NX
-        local_wait(bt.at[:, xb, :, 1 - c], sem_4.at[1 + d])
-        attend(xb)
-
-    block_in(1)
-    block_in(3)
-
-    block_use(1)
-    wide.a_step(4)
-    chip = x * NZ + z
-    for d in range(1, NZ):
-        remote(fac, fac_all.at[chip, c], sem_f.at[0], sem_f.at[1], (x, (z + d) % NZ, c, y))
-
-    to_plane(left_in, left_out, sem_g)
-    wide.y_step(7)
     block_in(2)
     block_use(3)
-    wide.far()
+    wide.a_step(4)
+    wide.y_step(7)
+
+    to_plane(left_in, left_out, sem_g)
+
     @pl.when(x != y)
     def _():
         local_wait(tgt_half, sem_t.at[3])
         remote(tgt_half, tgt_half, sem_t.at[6], sem_t.at[7], sibling)
 
     block_use(2)
+    wide.far()
     local_wait(fac_all.at[pl.ds(0, NZ - 1), c], sem_f.at[1])
     facs = fac_all.at[pl.ds(x * NZ, NZ), c]
     for d in range(1, NX):
@@ -566,8 +569,7 @@
             jax.ShapeDtypeStruct((ROWS, COLS), f32),
             jax.ShapeDtypeStruct((1, 128), f32),
         ),
-        in_specs=[pl.BlockSpec(memory_space=pltpu.SMEM)]
-        + [pl.BlockSpec(memory_space=pl.ANY)] * len(ins),
+        in_specs=[pl.BlockSpec(memory_space=pl.ANY)] * (1 + len(ins)),
         out_specs=[pl.BlockSpec(memory_space=pltpu.VMEM)] * 3,
         scratch_shapes=[pltpu.VMEM(held[i].shape, held[i].dtype) for i in order]
         + [
@@ -579,6 +581,7 @@
             pltpu.VMEM((NX * NZ, NC, 8, COLS), bf16),
             pltpu.VMEM((8, D), bf16),
             pltpu.VMEM((PLANE, 1, 128), f32),
+            pltpu.VMEM((1,), jnp.int32),
             pltpu.VMEM((NY, NZ, NC, ROWS, COLS + 128), bf16),
             pltpu.VMEM((NY, NX, NZ, NC, SLAB, tok), bf16),
             pltpu.VMEM((NY, 8, HEAD_DIM, tok), bf16),
@@ -591,7 +594,7 @@
             pltpu.VMEM((8, tok), bf16),
             pltpu.VMEM((NX, 1, 128), f32),
             pltpu.VMEM((1, 128), f32),
-            dma((12,)),
+            dma((13,)),
             dma((PlaneGather.SEMS,)),
             dma((2,)),
             dma((8,)),
@@ -608,6 +611,20 @@
             collective_id=0, has_side_effects=True, vmem_limit_bytes=60 * 1024 * 1024
         ),
     )(ids, *ins)
+
+
+def hand_on(*arrays):
+    def body(*refs):
+        for i in range(len(arrays)):
+            refs[len(arrays) + i][...] = refs[i][...]
+
+    return pl.pallas_call(
+        body,
+        name="hand_on",
+        out_shape=[jax.ShapeDtypeStruct(a.shape, a.dtype) for a in arrays],
+        in_specs=[pl.BlockSpec(memory_space=pltpu.VMEM)] * len(arrays),
+        out_specs=[pl.BlockSpec(memory_space=pltpu.VMEM)] * len(arrays),
+    )(*arrays)
 
 
 def tables(count, head_size):
@@ -647,6 +664,7 @@
         cos_t,
         sin_t,
     )
+    grad_q, grad_o, fit = hand_on(grad_q, grad_o, fit)
     return (grad_q, jnp.transpose(grad_o), fit[0, :1])
 
 

time: 79.4 us -> 73.4 us (0.924)
  local copies, waits for them, and re-layouts: 3.24 us -> 0 us
  between operations: 2.99 us -> 1.29 us
  Pallas kernels: 73 us -> 72 us
    unnamed x2 -> x0, local copies, waits for them, and re-layouts: 3.24 us -> none
    pallas_call x1, Pallas kernels: 73 us -> 70.2 us  [forward(): pl.pallas_call(forward_kernel, name='forward', out_shape=(jax.ShapeDtypeS...]
    pallas_call x0 -> x1, Pallas kernels: none -> 1.79 us  [hand_on(): pl.pallas_call(body, name='hand_on', out_shape=[jax.ShapeDtypeStruct(a.sh...]
where the time goes in v5:
time: 73.4 us; the launch traced here: 73.3 us
  Pallas kernels  72 us (98%)
  between operations  1.29 us (2%)
    pallas_call x1, Pallas kernels, forward(): pl.pallas_call(forward_kernel, name='forward', out_shape=(jax.ShapeDtypeS...  70.2 us
    pallas_call x1, Pallas kernels, hand_on(): pl.pallas_call(body, name='hand_on', out_shape=[jax.ShapeDtypeStruct(a.sh...  1.79 us

profile of v5, /device:TPU:1, one launch (start us, length us, event | category | flops | bytes accessed | tf_op | source)
XLA Modules:
  0.0 73.3 jit_solution(1357010373905165721)
XLA Ops:
  1.3 70.2 %forward.1 = (f32[56,896]{1,0:T(8,128)}, f32[56,896]{1,0:T(8,128)}, f32[1,128]{1,0:T(1,128)}) custom-call(s32[1]{0:T(128)S(6)} %copy.16.ids_h, bf16[256,3584]{1,0:T(8,128)(2,1)} %tok_h.1, bf16[3584,128]{1,0:T(8,128)(2,1)} %wk_h.1, bf16[3584,128]{1,0:T(8,128)(2,1)} %wv_h.1, bf16[56,896]{1,0:T(8,128)(2,1)} %bitcast.12, bf16[256,896]{1,0:T(8,128)(2,1)} %tgt_h.1, ...), custom_call_target="tpu_custom_call" | custom-call | tf_op jit(solution)/shard_map/forward/pallas_call | solution.py:564
  71.5 1.8 %hand_on.1 = (f32[56,896]{1,0:T(8,128)}, f32[56,896]{1,0:T(8,128)}, f32[1,128]{1,0:T(1,128)}) custom-call(f32[56,896]{1,0:T(8,128)} %get-tuple-element.9.refs_0_, f32[56,896]{1,0:T(8,128)} %get-tuple-element.10.refs_1_, f32[1,128]{1,0:T(1,128)} %get-tuple-element.11.refs_2_), custom_call_target="tpu_custom_call" | custom-call | tf_op jit(solution)/shard_map/hand_on/pallas_call | solution.py:621

commit v6 on v5

--- a/solution.py
+++ b/solution.py
@@ -176,7 +176,7 @@
     grad_q, grad_o, fit,
     tok, wk, wv, tgt, wq, ql, qr, ol, orr, cos, sin,
     slab_in, slab_out, left_in, left_out, fac, fac_all, lft, ev,
-    ids, wbuf, bt, mt, k4, v4, fb, lft_m, tgt_t, acc, low, part, total,
+    ids, wbuf, bt, mt, k4, v4, fb, lft_m, acc, low, part, total,
     sem_l, sem_w, sem_s, sem_t, sem_k, sem_1, sem_2, sem_3, sem_4, sem_f, sem_e, sem_g,
 ):
     me = place()
@@ -240,36 +240,37 @@
     )
     fac[...] = jnp.concatenate([qr[...].astype(f32), ol[...].astype(f32)], axis=0).astype(bf16)
     lft[...] = (jnp.concatenate([ql[...].astype(f32), orr[...].astype(f32)], axis=0) * sign).astype(bf16)
-    for i in range(PLANE):
-        left_in[i, :, pl.ds(0, ROWS)] = lft[:, pl.ds(i * ROWS, ROWS)]
     fb[:, :, pl.ds(COLS, 128)] = jnp.zeros((NY, 8, 128), bf16)
     slab_out[p] = slab_in[p]
-    left_out[p] = left_in[p]
     fac_all[x * NZ + z, c] = fac[...]
+
+    loads["wo"].wait()
+    loads["tgt"].wait()
+    pl.semaphore_wait(barrier, PLANE - 1 + 3 * NZ * NC + 9)
+
+    def to_plane(src, dst, sem):
+        for dx, dz, dc in PEERS:
+            xx, zz, cc = (x + dx) % NX, (z + dz) % NZ, (c + dc) % NC
+            remote(src.at[(xx * NZ + zz) * NC + cc], dst.at[p], sem.at[0], sem.at[1], (xx, zz, cc, y))
+
+    to_plane(slab_in, slab_out, sem_s)
+
+    @pl.when(x != y)
+    def _():
+        remote(lft, lft_m, sem_t.at[0], sem_t.at[1], (y, z, c, x))
+
+    wide = PlaneGather(me, wbuf, sem_w, CUT)
+    wide.start()
+
+    @pl.when(x == y)
+    def _():
+        lft_m[...] = lft[...]
 
     for name in ("tok", "wk", "wv", "cos", "sin"):
         loads[name].wait()
     key_t = jnp.dot(tok[...], wk[...], preferred_element_type=f32).T
     k4[y] = turned(key_t).T.astype(bf16)
     v4[y] = jnp.dot(tok[...], wv[...], preferred_element_type=f32).T.astype(bf16)
-    loads["wo"].wait()
-    loads["tgt"].wait()
-    pl.semaphore_wait(barrier, PLANE - 1 + 3 * NZ * NC + 9)
-
-    def to_plane(src, dst, sem):
-        for dx, dz, dc in PEERS:
-            xx, zz, cc = (x + dx) % NX, (z + dz) % NZ, (c + dc) % NC
-            remote(src.at[(xx * NZ + zz) * NC + cc], dst.at[p], sem.at[0], sem.at[1], (xx, zz, cc, y))
-
-    to_plane(slab_in, slab_out, sem_s)
-
-    @pl.when(x != y)
-    def _():
-        remote(lft, lft_m, sem_t.at[0], sem_t.at[1], (y, z, c, x))
-
-    wide = PlaneGather(me, wbuf, sem_w, CUT)
-    wide.start()
-
     key_half = k4.at[y, pl.ds(pl.multiple_of(c * 128, 128), 128)]
     value_half = v4.at[y, pl.ds(pl.multiple_of(c * 64, 64), 64)]
     for d in range(1, NY):
@@ -277,13 +278,19 @@
         remote(key_half, key_half, sem_k.at[0], sem_k.at[1], to)
         remote(value_half, value_half, sem_k.at[2], sem_k.at[3], to)
 
-    @pl.when(x == y)
-    def _():
-        lft_m[...] = lft[...]
+    for i in range(PLANE):
+        left_in[i, :, pl.ds(0, ROWS)] = lft[:, pl.ds(i * ROWS, ROWS)]
+    left_out[p] = left_in[p]
 
     @pl.when(x != y)
     def _():
         local_wait(lft_m, sem_t.at[1])
+
+    out_right = lft_m[pl.ds(RANK, RANK), pl.ds(pl.multiple_of(x * COLS, 128), COLS)].astype(f32)
+    beside = jnp.concatenate([out_right] * 3 + [jnp.zeros((128 - 3 * RANK, COLS), f32)], axis=0)
+    beside = beside.T.astype(bf16).reshape(NZ, NC, ROWS, 128)
+    for b in range(NY):
+        wbuf[b, :, :, :, pl.ds(COLS, 128)] = beside
 
     local_wait(slab_out.at[pl.ds(0, PLANE - 1)], sem_s.at[1])
     made = lax.dot_general(
@@ -324,14 +331,6 @@
         remote(line, line, sem_2.at[0], sem_2.at[d], (x, z, c, (y + d) % NY))
     line_out(y)
 
-    tgt_half = tgt.at[pl.ds(pl.multiple_of(c * 128, 128), 128)]
-
-    @pl.when(x == y)
-    def _():
-        for d in (2, 1, 3):
-            to = (x, z, c, (y + d) % NY)
-            remote(tgt_half, tgt_half, sem_t.at[2], sem_t.at[3], to)
-
     spot = fb.at[y, :, pl.ds(0, COLS)]
 
     @pl.when(x != y)
@@ -346,11 +345,13 @@
         fb[y, :, pl.ds(0, COLS)] = fac[...]
 
     local_wait(k4.at[pl.ds(0, 3), pl.ds(0, 128)], sem_k.at[1])
-    keys_in = k4.at[:, pl.ds(pl.multiple_of(c * 128, 128), 128)]
-    remote(keys_in, keys_in, sem_k.at[4], sem_k.at[5], sibling)
+    for d in range(1, NY):
+        keys_in = k4.at[(y + d) % NY, pl.ds(pl.multiple_of(c * 128, 128), 128)]
+        remote(keys_in, keys_in, sem_k.at[4], sem_k.at[5], sibling)
     local_wait(v4.at[pl.ds(0, 3), pl.ds(0, 64)], sem_k.at[3])
-    values_in = v4.at[:, pl.ds(pl.multiple_of(c * 64, 64), 64)]
-    remote(values_in, values_in, sem_k.at[7], sem_k.at[6], sibling)
+    for d in range(1, NY):
+        values_in = v4.at[(y + d) % NY, pl.ds(pl.multiple_of(c * 64, 64), 64)]
+        remote(values_in, values_in, sem_k.at[7], sem_k.at[6], sibling)
     for d in (1, 3, 2):
         yy = (y + NY - d) % NY
         local_wait(bt.at[yy, x, :, c], sem_2.at[d])
@@ -360,6 +361,14 @@
     wide.b_step(2)
     wide.y_step(1)
     wide.y_step(2)
+
+    tgt_half = tgt.at[pl.ds(pl.multiple_of(c * 128, 128), 128)]
+
+    @pl.when(x == y)
+    def _():
+        for d in (2, 1, 3):
+            to = (x, z, c, (y + d) % NY)
+            remote(tgt_half, tgt_half, sem_t.at[2], sem_t.at[3], to)
 
     row = lax.broadcasted_iota(jnp.int32, (tokens_n, tokens_n), 0)
     col = lax.broadcasted_iota(jnp.int32, (tokens_n, tokens_n), 1)
@@ -386,8 +395,8 @@
                     mt[yh, xb * 2 + j] = mixed.astype(bf16)
 
     local_wait(bt.at[:, x, :, 1 - c], sem_4.at[1])
-    local_wait(k4.at[:, pl.ds(0, 128)], sem_k.at[5])
-    local_wait(v4.at[:, pl.ds(0, 64)], sem_k.at[6])
+    local_wait(k4.at[pl.ds(0, 3), pl.ds(0, 128)], sem_k.at[5])
+    local_wait(v4.at[pl.ds(0, 3), pl.ds(0, 64)], sem_k.at[6])
 
     @pl.when(x != y)
     def _():
@@ -398,8 +407,8 @@
         local_wait(fb.at[pl.ds(0, 3), :, pl.ds(0, COLS)], sem_t.at[5])
 
     attend(x)
+    wide.a_step(2)
     wide.b_step(3)
-    wide.a_step(2)
     wide.y_step(3)
     wide.y_step(4)
 
@@ -445,20 +454,12 @@
     for d in range(1, NX):
         remote(facs, facs, sem_f.at[2], sem_f.at[3], ((x + d) % NX, z, c, y))
 
-    out_right = lft_m[pl.ds(RANK, RANK), pl.ds(pl.multiple_of(x * COLS, 128), COLS)].astype(f32)
-    beside = jnp.concatenate([out_right] * 3 + [jnp.zeros((128 - 3 * RANK, COLS), f32)], axis=0)
-    beside = beside.T.astype(bf16).reshape(NZ, NC, ROWS, 128)
-    for b in range(NY):
-        wbuf[b, :, :, :, pl.ds(COLS, 128)] = beside
-
     @pl.when(x != y)
     def _():
         local_wait(tgt.at[pl.ds(0, 128)], sem_t.at[7])
 
-    tgt_t[...] = tgt[...].astype(f32).T
-
     wide.finish()
-    acc[...] = -tgt_t[...]
+    acc[...] = -tgt[...].astype(f32).T
 
     @pl.loop(0, NY)
     def _(b):
@@ -482,8 +483,6 @@
     part[x] = jnp.full((1, 128), jnp.sum(acc[...] * acc[...]), f32)
     for d in range(1, NX):
         remote(part.at[x], part.at[x], sem_e.at[0], sem_e.at[1], ((x + d) % NX, z, c, y))
-    local_wait(fac_all.at[pl.ds(0, 3 * NZ), c], sem_f.at[3])
-    remote(fac_all.at[:, c], fac_all.at[:, c], sem_f.at[4], sem_f.at[5], sibling)
     local_wait(part.at[pl.ds(0, NX - 1)], sem_e.at[1])
     total[...] = part[0] + part[1] + part[2] + part[3]
     slot = (y * NZ + z) * NC + c
@@ -493,6 +492,8 @@
         to = (x, (z + dz) % NZ, (c + dc) % NC, (y + dy) % NY)
         remote(total, ev.at[slot], sem_e.at[2], sem_e.at[3], to)
 
+    local_wait(fac_all.at[pl.ds(0, 3 * NZ), c], sem_f.at[3])
+    remote(fac_all.at[:, c], fac_all.at[:, c], sem_f.at[4], sem_f.at[5], sibling)
     local_wait(left_out.at[pl.ds(0, PLANE - 1)], sem_g.at[1])
     local_wait(fac_all.at[:, 1 - c], sem_f.at[5])
     local_wait(ev.at[pl.ds(0, PLANE - 1)], sem_e.at[3])
@@ -542,8 +543,8 @@
 
     local_wait(k4.at[pl.ds(0, 3), pl.ds(0, 128)], sem_k.at[0])
     local_wait(v4.at[pl.ds(0, 3), pl.ds(0, 64)], sem_k.at[2])
-    local_wait(k4.at[:, pl.ds(0, 128)], sem_k.at[4])
-    local_wait(v4.at[:, pl.ds(0, 64)], sem_k.at[7])
+    local_wait(k4.at[pl.ds(0, 3), pl.ds(0, 128)], sem_k.at[4])
+    local_wait(v4.at[pl.ds(0, 3), pl.ds(0, 64)], sem_k.at[7])
     local_wait(bt.at[0, 0, pl.ds(0, 7), 0], sem_1.at[0])
     local_wait(bt.at[pl.ds(0, 3), 0, :, 0], sem_2.at[0])
     local_wait(bt.at[:, pl.ds(0, 3), :, 0], sem_3.at[0])
@@ -590,7 +591,6 @@
             pltpu.VMEM((NY, 8, COLS + 128), bf16),
             pltpu.VMEM((8, D), bf16),
             pltpu.VMEM((COLS, tok), f32),
-            pltpu.VMEM((COLS, tok), f32),
             pltpu.VMEM((8, tok), bf16),
             pltpu.VMEM((NX, 1, 128), f32),
             pltpu.VMEM((1, 128), f32),

time: 73.4 us -> 71 us (0.967)
  Pallas kernels: 72 us -> 69.6 us
    pallas_call x1, Pallas kernels: 70.2 us -> 67.8 us  [forward(): pl.pallas_call(forward_kernel, name='forward', out_shape=(jax.ShapeDtypeS...]
where the time goes in v6:
time: 71 us; the launch traced here: 70.9 us
  Pallas kernels  69.6 us (98%)
  between operations  1.29 us (2%)
    pallas_call x1, Pallas kernels, forward(): pl.pallas_call(forward_kernel, name='forward', out_shape=(jax.ShapeDtypeS...  67.8 us
    pallas_call x1, Pallas kernels, hand_on(): pl.pallas_call(body, name='hand_on', out_shape=[jax.ShapeDtypeStruct(a.sh...  1.79 us

profile of v6, /device:TPU:1, one launch (start us, length us, event | category | flops | bytes accessed | tf_op | source)
XLA Modules:
  0.0 70.9 jit_solution(17174166545078038617)
XLA Ops:
  1.3 67.8 %forward.1 = (f32[56,896]{1,0:T(8,128)}, f32[56,896]{1,0:T(8,128)}, f32[1,128]{1,0:T(1,128)}) custom-call(s32[1]{0:T(128)S(6)} %copy.16.ids_h, bf16[256,3584]{1,0:T(8,128)(2,1)} %tok_h.1, bf16[3584,128]{1,0:T(8,128)(2,1)} %wk_h.1, bf16[3584,128]{1,0:T(8,128)(2,1)} %wv_h.1, bf16[56,896]{1,0:T(8,128)(2,1)} %bitcast.12, bf16[256,896]{1,0:T(8,128)(2,1)} %tgt_h.1, ...), custom_call_target="tpu_custom_call" | custom-call | tf_op jit(solution)/shard_map/forward/pallas_call | solution.py:565
  69.1 1.8 %hand_on.1 = (f32[56,896]{1,0:T(8,128)}, f32[56,896]{1,0:T(8,128)}, f32[1,128]{1,0:T(1,128)}) custom-call(f32[56,896]{1,0:T(8,128)} %get-tuple-element.9.refs_0_, f32[56,896]{1,0:T(8,128)} %get-tuple-element.10.refs_1_, f32[1,128]{1,0:T(1,128)} %get-tuple-element.11.refs_2_), custom_call_target="tpu_custom_call" | custom-call | tf_op jit(solution)/shard_map/hand_on/pallas_call | solution.py:621
